TPU v7x, 512 devices: a whole 4x4x16 slice. The times are simulated.
512 devices in a mesh: cuts: 32 (over x, y, core), tr: 16 (over z).
Axes of the slice: x: 4, y: 4, z: 16, core: 2. Of those that a mesh axis runs over, the one named last changes fastest.
Arguments:
- cells: int32 [2, 32, 2, 1024], P(None, 'cuts'), may hold values from 1 to 509
- offsets: float32 [2, 32, 2, 1024], P(None, 'cuts'), may hold values from 0 to 1
- charges: float32 [2, 32, 1024], P(None, 'cuts'), may hold values from 0.5 to 2
- momenta: float32 [2, 32, 2, 1024], P(None, 'cuts', None, 'tr'), may hold values from -6 to 6
- green: float32 [1024, 1024], replicated, may hold values from -0.1875 to 0.1875
Outputs:
- momenta_out: float32 [2, 32, 2, 1024], P(None, 'cuts', None, 'tr')
Inputs may be any that keep to these rules, and one draw needn't show every extreme that they name: `cells`: every cell index lies in 1 .. 509.
All inputs are finite; a program needn't handle non-finite values.
Results may differ from a plain program's by a relative error of at most 0.017.
Values may be sent and summed in bfloat16 or wider, within the bound.
A program may use at most 64 MiB of HBM per device.

v0:
```python
import math

import jax
import jax.numpy as jnp
from jax import lax
from jax.sharding import PartitionSpec as P

SECTIONS = 4


drift_step = 0.5


def padded(cells, sides, width):
    for axis, dim in sides:
        count = lax.axis_size(axis)
        ends = count - 1
        head = lax.slice_in_dim(cells, 0, width, axis=dim)
        tail = lax.slice_in_dim(cells, cells.shape[dim] - width, cells.shape[dim], axis=dim)
        cells = jnp.concatenate(
            [
                lax.ppermute(tail, axis, [(i, (i + 1) % count) for i in range(ends)]),
                cells,
                lax.ppermute(head, axis, [((i + 1) % count, i) for i in range(ends)]),
            ],
            axis=dim,
        )
    return cells


def shifted(value, axis, steps):
    count = lax.axis_size(axis)
    pairs = [(source, (source + steps) % count) for source in range(count)]
    return lax.ppermute(value, axis, pairs)


def split_up(x, dim, count):
    shape = x.shape
    tiles = x.reshape(*shape[:dim], count, shape[dim] // count, *shape[dim + 1 :])
    return jnp.moveaxis(tiles, dim, 0)


def sent_and_summed(x, axis, dim):
    count = lax.axis_size(axis)
    tiles = lax.all_to_all(split_up(x, dim, count), axis, 0, 0, tiled=True)
    return jnp.sum(tiles, axis=0)


def in_order(tiles, dim):
    shape = list(tiles.shape[1:])
    shape[dim] *= tiles.shape[0]
    return jnp.moveaxis(tiles, 0, dim).reshape(shape)


def copy_for_each(x, axis):
    count = lax.axis_size(axis)
    return lax.all_to_all(jnp.broadcast_to(x[None], (count, *x.shape)), axis, 0, 0, tiled=True)


def gather_directly(x, axis, dim):
    return in_order(copy_for_each(x, axis), dim)


def phase_angles(frequency, position, period):
    return 2.0 * math.pi / period * (frequency * position % period).astype(jnp.float32)


def column_table(inputs, with_imag, begin_col, col_count, piece_width, period):
    columns = begin_col + lax.iota(jnp.int32, col_count)
    halves = columns // piece_width % 2
    frequency = columns // (2 * piece_width) * piece_width + columns % piece_width
    position = lax.iota(jnp.int32, inputs)[:, None]
    theta = phase_angles(frequency[None, :], position, period)
    cosine = jnp.cos(theta)
    sine = jnp.sin(theta)
    table = jnp.where(halves[None, :] == 0, cosine, -sine)
    if with_imag:
        lower = jnp.where(halves[None, :] == 0, sine, cosine)
        table = jnp.concatenate([table, lower], axis=0)
    return table.astype(jnp.bfloat16)


def row_table(inputs, period):
    theta = phase_angles(
        lax.iota(jnp.int32, period)[:, None], lax.iota(jnp.int32, inputs)[None, :], period
    )
    return jnp.concatenate([jnp.cos(theta), jnp.sin(theta)], axis=0).astype(jnp.bfloat16)


def forward_rows(table, spectrum, piece_width):
    both_parts = jnp.dot(table, spectrum, preferred_element_type=jnp.float32)
    period = table.shape[0] // 2
    cosine_part = both_parts[:period]
    sine_part = both_parts[period:]
    real_part = cosine_part[:, :piece_width] + sine_part[:, piece_width:]
    imag_part = cosine_part[:, piece_width:] - sine_part[:, :piece_width]
    return (real_part, imag_part)


def hat_weights(cells_along, fraction, first_node, node_count):
    nodes = first_node + lax.iota(jnp.int32, node_count)[None, :]
    lower = jnp.where(cells_along[:, None] == nodes, 1.0 - fraction[:, None], 0.0)
    upper = jnp.where(cells_along[:, None] + 1 == nodes, fraction[:, None], 0.0)
    return lower + upper


def deposit(cells, offsets, charges, first_node, node_rows, node_cols):
    particles = cells.shape[1]
    block_size = math.gcd(particles, 512)
    grid_sum = jnp.zeros((node_rows, node_cols), jnp.float32)
    for number in range(particles // block_size):
        begin_at = number * block_size
        finish_at = begin_at + block_size
        weight_rows = hat_weights(
            cells[0, begin_at:finish_at], offsets[0, begin_at:finish_at], first_node, node_rows
        )
        weight_cols = hat_weights(
            cells[1, begin_at:finish_at], offsets[1, begin_at:finish_at], 0, node_cols
        )
        weight_cols = charges[begin_at:finish_at][:, None] * weight_cols
        grid_sum = grid_sum + lax.dot_general(
            weight_rows.astype(jnp.bfloat16),
            weight_cols.astype(jnp.bfloat16),
            (((0,), (0,)), ((), ())),
            preferred_element_type=jnp.float32,
        )
    return grid_sum.astype(jnp.bfloat16)


def drift(cells, offsets, moment, extent):
    place = cells.astype(jnp.float32) + offsets + drift_step * moment
    place = jnp.clip(place, 1.0, extent - 2.0 - 1.0 / 64.0)
    whole = jnp.floor(place)
    return (whole.astype(jnp.int32), place - whole)


def potentials(pair_grid, pair_columns, own_columns, pair_rows, kernel_re, kernel_im, piece_width):
    spectrum = jnp.dot(pair_grid, own_columns, preferred_element_type=jnp.float32).astype(
        jnp.bfloat16
    )
    forward_re, forward_im = forward_rows(pair_rows, spectrum, piece_width)
    scaled = jnp.concatenate(
        [
            forward_re * kernel_re - forward_im * kernel_im,
            forward_re * kernel_im + forward_im * kernel_re,
        ],
        axis=1,
    ).astype(jnp.bfloat16)
    period = pair_rows.shape[0] // 2
    extent = pair_rows.shape[1]
    halves = lax.dot_general(
        pair_rows.reshape(2, period, extent),
        scaled,
        (((1,), (0,)), ((), ())),
        preferred_element_type=jnp.float32,
    )
    cosine_part = halves[0]
    sine_part = halves[1]
    inverse = jnp.concatenate(
        [
            cosine_part[:, :piece_width] - sine_part[:, piece_width:],
            cosine_part[:, piece_width:] + sine_part[:, :piece_width],
        ],
        axis=1,
    ).astype(jnp.bfloat16)
    inverse = lax.all_to_all(inverse, "tr", split_axis=0, concat_axis=1, tiled=True)
    potential = lax.dot_general(
        inverse, pair_columns, (((1,), (1,)), ((), ())), preferred_element_type=jnp.float32
    ) * (1.0 / (period * period))
    return potential.reshape(potential.shape[0], 2, extent)


def field_grids(potential):
    widened = padded(potential.astype(jnp.bfloat16), (("tr", 0),), 1).astype(potential.dtype)
    along_rows = (widened[:-2] - widened[2:]) * 0.5
    sideways = jnp.pad(potential, ((0, 0), (0, 0), (1, 1)))
    along_cols = (sideways[:, :, :-2] - sideways[:, :, 2:]) * 0.5
    stacked = jnp.stack([along_rows, along_cols], axis=0)
    node_rows = potential.shape[0]
    return (
        jnp.transpose(stacked, (2, 0, 1, 3))
        .reshape(2, 2 * node_rows, potential.shape[2])
        .astype(jnp.bfloat16)
    )


def kick_terms(cells, offsets, fields, first_node, node_rows, row_count):
    node_cols = fields.shape[2]
    block_size = math.gcd(row_count, 256)

    def one_block(number):
        begin_at = number * block_size
        columns = []
        for beam_index in range(2):
            row_cells = lax.dynamic_slice_in_dim(cells[beam_index, 0], begin_at, block_size)
            col_cells = lax.dynamic_slice_in_dim(cells[beam_index, 1], begin_at, block_size)
            row_frac = lax.dynamic_slice_in_dim(offsets[beam_index, 0], begin_at, block_size)
            col_frac = lax.dynamic_slice_in_dim(offsets[beam_index, 1], begin_at, block_size)
            weight_rows = hat_weights(row_cells, row_frac, first_node, node_rows).astype(
                jnp.bfloat16
            )
            weight_cols = hat_weights(col_cells, col_frac, 0, node_cols).astype(jnp.bfloat16)
            projected = lax.dot_general(
                weight_cols,
                fields[1 - beam_index],
                (((1,), (1,)), ((), ())),
                preferred_element_type=jnp.float32,
            )
            projected = projected.reshape(block_size, 2, node_rows)
            columns.append(jnp.sum(projected * weight_rows.astype(jnp.float32)[:, None, :], axis=2))
        return jnp.concatenate(columns, axis=1)

    blocks = lax.map(one_block, jnp.arange(row_count // block_size, dtype=jnp.int32))
    return blocks.reshape(row_count, 4)


def per_device(cells, offsets, charges, momenta, green):
    shards = lax.axis_size("tr")
    shard_index = lax.axis_index("tr")
    period = green.shape[0]
    extent = period // 2
    node_rows = extent // shards
    piece_width = period // shards
    first_node = shard_index * node_rows
    kernel_columns = column_table(
        period, False, shard_index * 2 * piece_width, 2 * piece_width, piece_width, period
    )
    kernel_cols = jnp.dot(
        green.astype(jnp.bfloat16), kernel_columns, preferred_element_type=jnp.float32
    ).astype(jnp.bfloat16)
    kernel_re, kernel_im = forward_rows(row_table(period, period), kernel_cols, piece_width)
    pair_columns = column_table(extent, True, 0, 2 * period, piece_width, period)
    pair_rows = row_table(extent, period)
    own_columns = column_table(
        extent, True, shard_index * 2 * piece_width, 2 * piece_width, piece_width, period
    )
    deposit_first = 0
    local_cells = cells[:, 0]
    local_offsets = offsets[:, 0]
    local_charges = charges[:, 0]
    moment = momenta
    particle_rows = momenta.shape[-1]
    for section_index in range(SECTIONS):
        charge_grids = [
            deposit(
                local_cells[beam_index],
                local_offsets[beam_index],
                local_charges[beam_index],
                deposit_first,
                extent,
                extent,
            )
            for beam_index in range(2)
        ]
        if section_index > 0:
            charge_grids = [
                shifted(charge_grids[0], "cuts", 2 * section_index),
                shifted(charge_grids[1], "cuts", -2 * section_index),
            ]
        pair_grid = jnp.concatenate(charge_grids, axis=1)
        potential = potentials(
            pair_grid, pair_columns, own_columns, pair_rows, kernel_re, kernel_im, piece_width
        )
        fields = field_grids(potential)
        kick_sums = sent_and_summed(
            kick_terms(
                local_cells,
                local_offsets,
                fields,
                first_node,
                node_rows,
                particle_rows * lax.axis_size("tr"),
            ),
            "tr",
            0,
        )
        moment = moment + jnp.transpose(kick_sums).reshape(moment.shape)
        if section_index + 1 < SECTIONS:
            whole_moment = gather_directly(moment, "tr", 3)
            local_cells, local_offsets = drift(
                local_cells, local_offsets, whole_moment[:, 0], extent
            )
    return moment


def solution(mesh):
    return jax.shard_map(
        per_device,
        mesh=mesh,
        in_specs=(
            P(None, "cuts", None, None),
            P(None, "cuts", None, None),
            P(None, "cuts", None),
            P(None, "cuts", None, "tr"),
            P(),
        ),
        out_specs=P(None, "cuts", None, "tr"),
        check_vma=False,
    )
```

profile of v0, /device:TPU:6, one launch (start us, length us, event | category | flops | bytes accessed | tf_op | source)
XLA Modules:
  0.0 439.2 jit_solution(6951870104126059463)
XLA Ops:
  0.0 8.5 %fusion.147 = (bf16[1024,512]{1,0:T(8,128)(2,1)S(1)}, bf16[1024,512]{1,0:T(8,128)(2,1)S(1)}) fusion(), kind=kLoop, calls=%fused_computation.362 | loop fusion | flops 8388608 | bytes 2097152 | tf_op jit(solution)/shard_map/sin | solution.py:87
  8.6 17.7 %sine_convert_fusion = (bf16[1024,1024]{1,0:T(8,128)(2,1)}, bf16[1024,1024]{1,0:T(8,128)(2,1)}) fusion(), kind=kLoop, calls=%fused_computation.206 | loop fusion | flops 16777216 | bytes 4194304 | tf_op jit(solution)/shard_map/convert.43
  28.4 8.5 %fusion.86 = f32[2048,128]{0,1:T(8,128)} fusion(bf16[1024,1024]{1,0:T(8,128)(2,1)} %get-tuple-element.438, bf16[1024,1024]{1,0:T(8,128)(2,1)} %get-tuple-element.439, f32[1024,1024]{1,0:T(8,128)} %param.17, s32[128]{0:T(128)S(1)} %fusion.412, pred[128]{0:T(512)(128)(4,1)S(1)} %fusion.413), kind=kOutput, calls=%fused_computation.197 | convolution fusion | flops 817102848 | bytes 9437824 | tf_op jit(solution)/shard_map/dot_general | solution.py:91
  49.4 15.4 %all-to-all-start = ((bf16[16,32,128]{2,1,0:T(8,128)(2,1)}), bf16[16,32,128]{2,1,0:T(8,128)(2,1)S(1)}, u32[]{:S(2)}, u32[]{:S(2)}) async-start(bf16[16,32,128]{2,1,0:T(8,128)(2,1)} %pad_maximum_fusion.2), calls=%async_computation | async-start | bytes 262144 | tf_op jit(solution)/shard_map/all_to_all | solution.py:166
  64.8 18.5 %select_convert_fusion.1 = (bf16[512,2048]{1,0:T(8,128)(2,1)}, bf16[512,2048]{1,0:T(8,128)(2,1)}) fusion(s32[2048]{0:T(1024)S(1)} %fusion.409, pred[2048]{0:T(1024)(128)(4,1)S(1)} %fusion.406), kind=kLoop, calls=%fused_computation.203 | loop fusion | flops 19922944 | bytes 4204544 | tf_op jit(solution)/shard_map/convert.34
  97.2 9.5 %while.40 = (s32[]{:T(128)}, f32[4,256,4]{1,0,2:T(4,128)S(1)}, s32[2,2,1024]{2,1,0:T(2,128)S(1)}, s32[4]{0:T(128)S(1)}, f32[2,2,1024]{2,1,0:T(2,128)S(1)}, /*ind...) while((s32[]{:T(128)}, f32[4,256,4]{1,0,2:T(4,128)S(1)}, ...), condition=%wide.region_3.4_spmd, body=%wide.region_0.3_spmd.sunk | while | flops 35309604 | bytes 668095 | solution.py:213
  106.9 24.2 %all_to_all.99 = f32[16,1,256]{2,1,0:T(1,128)S(1)} all-to-all(f32[16,1,256]{2,1,0:T(1,128)S(1)} %reshape.1728), channel_id=1, replica_groups=mesh['cuts'=32,'tr'=16] {'tr'}, dimensions={0} | all-to-all | bytes 32768 | tf_op jit(solution)/shard_map/all_to_all | solution.py:45
  132.5 15.0 %all_to_all.100 = f32[16,1,256]{2,1,0:T(1,128)S(1)} all-to-all(f32[16,1,256]{2,1,0:T(1,128)S(1)} %reshape.1730), channel_id=1, replica_groups=mesh['cuts'=32,'tr'=16] {'tr'}, dimensions={0} | all-to-all | bytes 32768 | tf_op jit(solution)/shard_map/all_to_all | solution.py:57
  156.9 4.6 %collective-permute-start.3 = (bf16[512,512]{1,0:T(8,128)(2,1)S(1)}, bf16[512,512]{1,0:T(8,128)(2,1)}, u32[]{:S(2)}, u32[]{:S(2)}) collective-permute-start(bf16[512,512]{1,0:T(8,128)(2,1)S(1)} %fusion.109), channel_id=1, source_target_pairs={{0,480},{16,496},{32,0},{48,16},{64,32},{80,48},{96,64},{112,80},{... | collective-permute-start | bytes 1572872 | tf_op jit(solution)/shard_map/ppermute | solution.py:34
  174.3 16.0 %all_to_all.101 = bf16[16,32,128]{2,1,0:T(8,128)(2,1)S(1)} all-to-all(bf16[16,32,128]{2,1,0:T(8,128)(2,1)S(1)} %pad_maximum_fusion.3), channel_id=1, replica_groups=mesh['cuts'=32,'tr'=16] {'tr'}, dimensions={0} | all-to-all | bytes 262144 | tf_op jit(solution)/shard_map/all_to_all | solution.py:166
  203.3 9.6 %while.41 = (s32[]{:T(128)}, f32[4,256,4]{1,0,2:T(4,128)S(1)}, s32[2,2,1024]{2,1,0:T(2,128)S(1)}, s32[4]{0:T(128)S(1)}, f32[2,2,1024]{2,1,0:T(2,128)S(1)}, /*ind...) while((s32[]{:T(128)}, f32[4,256,4]{1,0,2:T(4,128)S(1)}, ...), condition=%wide.region_8.9_spmd, body=%wide.region_5.8_spmd.sunk | while | flops 35309604 | bytes 668095 | solution.py:213
  213.1 18.5 %all_to_all.102 = f32[16,1,256]{2,1,0:T(1,128)S(1)} all-to-all(f32[16,1,256]{2,1,0:T(1,128)S(1)} %reshape.1732), channel_id=1, replica_groups=mesh['cuts'=32,'tr'=16] {'tr'}, dimensions={0} | all-to-all | bytes 32768 | tf_op jit(solution)/shard_map/all_to_all | solution.py:45
  232.5 15.0 %all_to_all.103 = f32[16,1,256]{2,1,0:T(1,128)S(1)} all-to-all(f32[16,1,256]{2,1,0:T(1,128)S(1)} %reshape.1734), channel_id=1, replica_groups=mesh['cuts'=32,'tr'=16] {'tr'}, dimensions={0} | all-to-all | bytes 32768 | tf_op jit(solution)/shard_map/all_to_all | solution.py:57
  250.9 4.8 %collective-permute-start.6 = (bf16[512,512]{1,0:T(8,128)(2,1)S(1)}, bf16[512,512]{1,0:T(8,128)(2,1)}, u32[]{:S(2)}, u32[]{:S(2)}) collective-permute-start(bf16[512,512]{1,0:T(8,128)(2,1)S(1)} %fusion.110), channel_id=1, source_target_pairs={{0,64},{16,80},{32,96},{48,112},{64,128},{80,144},{96,160},{112,17... | collective-permute-start | bytes 1572872 | tf_op jit(solution)/shard_map/ppermute | solution.py:34
  264.5 6.4 %collective-permute-done.7 = bf16[512,512]{1,0:T(8,128)(2,1)} collective-permute-done((bf16[512,512]{1,0:T(8,128)(2,1)S(1)}, bf16[512,512]{1,0:T(8,128)(2,1)}, u32[]{:S(2)}, u32[]{:S(2)}) %collective-permute-start.7) | collective-permute-done | bytes 524320 | tf_op jit(solution)/shard_map/ppermute | solution.py:34
  276.9 15.7 %all_to_all.104 = bf16[16,32,128]{2,1,0:T(8,128)(2,1)S(1)} all-to-all(bf16[16,32,128]{2,1,0:T(8,128)(2,1)S(1)} %pad_maximum_fusion.4), channel_id=1, replica_groups=mesh['cuts'=32,'tr'=16] {'tr'}, dimensions={0} | all-to-all | bytes 262144 | tf_op jit(solution)/shard_map/all_to_all | solution.py:166
  305.6 9.8 %while.42 = (s32[]{:T(128)}, f32[4,256,4]{1,0,2:T(4,128)S(1)}, s32[2,2,1024]{2,1,0:T(2,128)S(1)}, s32[4]{0:T(128)S(1)}, f32[2,2,1024]{2,1,0:T(2,128)S(1)}, /*ind...) while((s32[]{:T(128)}, f32[4,256,4]{1,0,2:T(4,128)S(1)}, ...), condition=%wide.region_13.14_spmd, body=%wide.region_10.13_spmd.sunk | while | flops 35309604 | bytes 668095 | solution.py:213
  315.6 18.7 %all_to_all.105 = f32[16,1,256]{2,1,0:T(1,128)S(1)} all-to-all(f32[16,1,256]{2,1,0:T(1,128)S(1)} %reshape.1736), channel_id=1, replica_groups=mesh['cuts'=32,'tr'=16] {'tr'}, dimensions={0} | all-to-all | bytes 32768 | tf_op jit(solution)/shard_map/all_to_all | solution.py:45
  335.2 15.0 %all_to_all.106 = f32[16,1,256]{2,1,0:T(1,128)S(1)} all-to-all(f32[16,1,256]{2,1,0:T(1,128)S(1)} %reshape.1738), channel_id=1, replica_groups=mesh['cuts'=32,'tr'=16] {'tr'}, dimensions={0} | all-to-all | bytes 32768 | tf_op jit(solution)/shard_map/all_to_all | solution.py:57
  353.5 6.0 %collective-permute-start.10 = (bf16[512,512]{1,0:T(8,128)(2,1)S(1)}, bf16[512,512]{1,0:T(8,128)(2,1)S(1)}, u32[]{:S(2)}, u32[]{:S(2)}) collective-permute-start(bf16[512,512]{1,0:T(8,128)(2,1)S(1)} %fusion.112), channel_id=1, source_target_pairs={{0,96},{16,112},{32,128},{48,144},{64,160},{80,176},{96,192},{112,... | collective-permute-start | bytes 1572872 | tf_op jit(solution)/shard_map/ppermute | solution.py:34
  366.2 8.2 %collective-permute-done.11 = bf16[512,512]{1,0:T(8,128)(2,1)} collective-permute-done((bf16[512,512]{1,0:T(8,128)(2,1)S(1)}, bf16[512,512]{1,0:T(8,128)(2,1)}, u32[]{:S(2)}, u32[]{:S(2)}) %collective-permute-start.11) | collective-permute-done | bytes 524320 | tf_op jit(solution)/shard_map/ppermute | solution.py:34
  380.4 15.8 %all_to_all.107 = bf16[16,32,128]{2,1,0:T(8,128)(2,1)S(1)} all-to-all(bf16[16,32,128]{2,1,0:T(8,128)(2,1)S(1)} %pad_maximum_fusion.5), channel_id=1, replica_groups=mesh['cuts'=32,'tr'=16] {'tr'}, dimensions={0} | all-to-all | bytes 262144 | tf_op jit(solution)/shard_map/all_to_all | solution.py:166
  408.5 10.0 %while.43 = (s32[]{:T(128)}, f32[4,256,4]{1,0,2:T(4,128)S(1)}, s32[2,2,1024]{2,1,0:T(2,128)S(1)}, s32[4]{0:T(128)S(1)}, f32[2,2,1024]{2,1,0:T(2,128)S(1)}, /*ind...) while((s32[]{:T(128)}, f32[4,256,4]{1,0,2:T(4,128)S(1)}, ...), condition=%wide.region_18.19_spmd, body=%wide.region_15.18_spmd.sunk | while | flops 35309604 | bytes 668095 | solution.py:213
  418.7 18.7 %all_to_all.108 = f32[16,1,256]{2,1,0:T(1,128)S(1)} all-to-all(f32[16,1,256]{2,1,0:T(1,128)S(1)} %reshape.1740), channel_id=1, replica_groups=mesh['cuts'=32,'tr'=16] {'tr'}, dimensions={0} | all-to-all | bytes 32768 | tf_op jit(solution)/shard_map/all_to_all | solution.py:45
  (666 shorter events, 152.4 us)
Async XLA Ops:
  8.5 17.8 %copy-start.5 = (s32[2,1,2,1024]{3,2,1,0:T(2,128)S(1)}, s32[2,1,2,1024]{3,2,1,0:T(2,128)}, u32[]{:S(2)}) copy-start(s32[2,1,2,1024]{3,2,1,0:T(2,128)} %param.13) | copy-start | bytes 49156
  8.5 17.8 %copy-start.6 = (f32[2,1,2,1024]{3,2,1,0:T(2,128)S(1)}, f32[2,1,2,1024]{3,2,1,0:T(2,128)}, u32[]{:S(2)}) copy-start(f32[2,1,2,1024]{3,2,1,0:T(2,128)} %param.14) | copy-start | bytes 49156
  8.6 17.9 %copy-start.8 = (f32[2,1,1024]{2,1,0:T(1,128)S(1)}, f32[2,1,1024]{2,1,0:T(1,128)}, u32[]{:S(2)}) copy-start(f32[2,1,1024]{2,1,0:T(1,128)} %param.15) | copy-start | bytes 24580
  26.5 14.9 %copy-start.10 = (f32[1,1,512]{2,1,0:T(1,128)}, f32[1,1,512]{2,1,0:T(1,128)S(1)}, u32[]{:S(2)}) copy-start(f32[1,1,512]{2,1,0:T(1,128)S(1)} %get-tuple-element.416) | copy-start | bytes 6148
  28.3 15.1 %copy-start.2 = (bf16[512,128]{1,0:T(8,128)(2,1)}, bf16[512,128]{1,0:T(8,128)(2,1)S(1)}, u32[]{:S(2)}) copy-start(bf16[512,128]{1,0:T(8,128)(2,1)S(1)} %get-tuple-element.427) | copy-start | bytes 393220
  49.4 33.9 %all-to-all-start = ((bf16[16,32,128]{2,1,0:T(8,128)(2,1)}), bf16[16,32,128]{2,1,0:T(8,128)(2,1)S(1)}, u32[]{:S(2)}, u32[]{:S(2)}) async-start(bf16[16,32,128]{2,1,0:T(8,128)(2,1)} %pad_maximum_fusion.2), calls=%async_computation | async-start | bytes 262144 | tf_op jit(solution)/shard_map/all_to_all | solution.py:166
  87.3 5.2 %collective-permute-start = (bf16[1,2,512]{2,1,0:T(2,128)(2,1)S(1)}, bf16[1,2,512]{2,1,0:T(2,128)(2,1)S(1)}, u32[]{:S(2)}, u32[]{:S(2)}) collective-permute-start(bf16[1,2,512]{2,1,0:T(2,128)(2,1)S(1)} %get-tuple-element.338), channel_id=1, source_target_pairs={{0,1},{1,2},{2,3},{3,4},{4,5},{5,6},{6,7},{7,8},{8,9},{9,10},{10,1... | collective-permute-start | bytes 6152 | tf_op jit(solution)/shard_map/ppermute | solution.py:22
  91.3 5.5 %collective-permute-start.1 = (bf16[1,2,512]{2,1,0:T(2,128)(2,1)S(1)}, bf16[1,2,512]{2,1,0:T(2,128)(2,1)S(1)}, u32[]{:S(2)}, u32[]{:S(2)}) collective-permute-start(bf16[1,2,512]{2,1,0:T(2,128)(2,1)S(1)} %get-tuple-element.339), channel_id=1, source_target_pairs={{1,0},{2,1},{3,2},{4,3},{5,4},{6,5},{7,6},{8,7},{9,8},{10,9},{11,1... | collective-permute-start | bytes 6152 | tf_op jit(solution)/shard_map/ppermute | solution.py:24
  97.1 35.3 %copy-start.9 = (f32[2,1,2,64]{3,2,1,0:T(2,128)S(1)}, f32[2,1,2,64]{3,2,1,0:T(2,128)}, u32[]{:S(2)}) copy-start(f32[2,1,2,64]{3,2,1,0:T(2,128)} %param.16) | copy-start | bytes 3076
  97.2 51.4 %copy-start.17 = (f32[1,1,512]{2,1,0:T(1,128)S(1)}, f32[1,1,512]{2,1,0:T(1,128)}, u32[]{:S(2)}) copy-start(f32[1,1,512]{2,1,0:T(1,128)} %copy-done.16) | copy-start | bytes 6148
  150.9 13.3 %collective-permute-start.2 = (bf16[512,512]{1,0:T(8,128)(2,1)S(1)}, bf16[512,512]{1,0:T(8,128)(2,1)}, u32[]{:S(2)}, u32[]{:S(2)}) collective-permute-start(bf16[512,512]{1,0:T(8,128)(2,1)S(1)} %fusion.108), channel_id=1, source_target_pairs={{0,32},{16,48},{32,64},{48,80},{64,96},{80,112},{96,128},{112,144}... | collective-permute-start | bytes 1572872 | tf_op jit(solution)/shard_map/ppermute | solution.py:34
  156.9 15.2 %copy-start.1 = (f32[1024,64]{0,1:T(8,128)S(1)}, f32[1024,64]{0,1:T(8,128)}, u32[]{:S(2)}) copy-start(f32[1024,64]{0,1:T(8,128)} %copy-done) | copy-start | bytes 786436
  156.9 11.3 %collective-permute-start.3 = (bf16[512,512]{1,0:T(8,128)(2,1)S(1)}, bf16[512,512]{1,0:T(8,128)(2,1)}, u32[]{:S(2)}, u32[]{:S(2)}) collective-permute-start(bf16[512,512]{1,0:T(8,128)(2,1)S(1)} %fusion.109), channel_id=1, source_target_pairs={{0,480},{16,496},{32,0},{48,16},{64,32},{80,48},{96,64},{112,80},{... | collective-permute-start | bytes 1572872 | tf_op jit(solution)/shard_map/ppermute | solution.py:34
  194.4 4.3 collective-permute-start.4
  197.4 5.5 %collective-permute-start.5 = (bf16[1,2,512]{2,1,0:T(2,128)(2,1)S(1)}, bf16[1,2,512]{2,1,0:T(2,128)(2,1)S(1)}, u32[]{:S(2)}, u32[]{:S(2)}) collective-permute-start(bf16[1,2,512]{2,1,0:T(2,128)(2,1)S(1)} %get-tuple-element.337), channel_id=1, source_target_pairs={{1,0},{2,1},{3,2},{4,3},{5,4},{6,5},{7,6},{8,7},{9,8},{10,9},{11,1... | collective-permute-start | bytes 6152 | tf_op jit(solution)/shard_map/ppermute | solution.py:24
  250.9 13.6 %collective-permute-start.6 = (bf16[512,512]{1,0:T(8,128)(2,1)S(1)}, bf16[512,512]{1,0:T(8,128)(2,1)}, u32[]{:S(2)}, u32[]{:S(2)}) collective-permute-start(bf16[512,512]{1,0:T(8,128)(2,1)S(1)} %fusion.110), channel_id=1, source_target_pairs={{0,64},{16,80},{32,96},{48,112},{64,128},{80,144},{96,160},{112,17... | collective-permute-start | bytes 1572872 | tf_op jit(solution)/shard_map/ppermute | solution.py:34
  258.2 12.7 %collective-permute-start.7 = (bf16[512,512]{1,0:T(8,128)(2,1)S(1)}, bf16[512,512]{1,0:T(8,128)(2,1)}, u32[]{:S(2)}, u32[]{:S(2)}) collective-permute-start(bf16[512,512]{1,0:T(8,128)(2,1)S(1)} %fusion.111), channel_id=1, source_target_pairs={{0,448},{16,464},{32,480},{48,496},{64,0},{80,16},{96,32},{112,48}... | collective-permute-start | bytes 1572872 | tf_op jit(solution)/shard_map/ppermute | solution.py:34
  296.7 4.3 collective-permute-start.8
  299.7 5.5 %collective-permute-start.9 = (bf16[1,2,512]{2,1,0:T(2,128)(2,1)S(1)}, bf16[1,2,512]{2,1,0:T(2,128)(2,1)S(1)}, u32[]{:S(2)}, u32[]{:S(2)}) collective-permute-start(bf16[1,2,512]{2,1,0:T(2,128)(2,1)S(1)} %get-tuple-element.335), channel_id=1, source_target_pairs={{1,0},{2,1},{3,2},{4,3},{5,4},{6,5},{7,6},{8,7},{9,8},{10,9},{11,1... | collective-permute-start | bytes 6152 | tf_op jit(solution)/shard_map/ppermute | solution.py:24
  353.5 12.7 %collective-permute-start.10 = (bf16[512,512]{1,0:T(8,128)(2,1)S(1)}, bf16[512,512]{1,0:T(8,128)(2,1)S(1)}, u32[]{:S(2)}, u32[]{:S(2)}) collective-permute-start(bf16[512,512]{1,0:T(8,128)(2,1)S(1)} %fusion.112), channel_id=1, source_target_pairs={{0,96},{16,112},{32,128},{48,144},{64,160},{80,176},{96,192},{112,... | collective-permute-start | bytes 1572872 | tf_op jit(solution)/shard_map/ppermute | solution.py:34
  362.0 12.4 %collective-permute-start.11 = (bf16[512,512]{1,0:T(8,128)(2,1)S(1)}, bf16[512,512]{1,0:T(8,128)(2,1)}, u32[]{:S(2)}, u32[]{:S(2)}) collective-permute-start(bf16[512,512]{1,0:T(8,128)(2,1)S(1)} %fusion.113), channel_id=1, source_target_pairs={{0,416},{16,432},{32,448},{48,464},{64,480},{80,496},{96,0},{112,1... | collective-permute-start | bytes 1572872 | tf_op jit(solution)/shard_map/ppermute | solution.py:34
  379.9 16.3 %copy-start.4 = (bf16[512,2048]{1,0:T(8,128)(2,1)S(1)}, bf16[512,2048]{1,0:T(8,128)(2,1)}, u32[]{:S(2)}) copy-start(bf16[512,2048]{1,0:T(8,128)(2,1)} %get-tuple-element.356) | copy-start | bytes 6291460
  399.6 4.3 collective-permute-start.12
  402.6 5.5 %collective-permute-start.13 = (bf16[1,2,512]{2,1,0:T(2,128)(2,1)S(1)}, bf16[1,2,512]{2,1,0:T(2,128)(2,1)S(1)}, u32[]{:S(2)}, u32[]{:S(2)}) collective-permute-start(bf16[1,2,512]{2,1,0:T(2,128)(2,1)S(1)} %get-tuple-element.333), channel_id=1, source_target_pairs={{1,0},{2,1},{3,2},{4,3},{5,4},{6,5},{7,6},{8,7},{9,8},{10,9},{11,1... | collective-permute-start | bytes 6152 | tf_op jit(solution)/shard_map/ppermute | solution.py:24
  (9 other events, 69.5 us)
where the time goes:
time: 443 us; the launch traced here: 439 us
  blocking collectives  172 us (39%)
  matrix products  69.9 us (16%)
  other arithmetic  63.5 us (14%)
  starting transfers between devices  57.8 us (13%)
  waiting for transfers between devices  43.1 us (10%)
  local copies, waits for them, and re-layouts  16.7 us (4%)
  loops' own time  13.4 us (3%)
    all_to_all x4, blocking collectives, sent_and_summed(): tiles = lax.all_to_all(split_up(x, dim, count), axis, 0, 0, tiled=True)  80.1 us
    all_to_all x3, blocking collectives, potentials(): lax.all_to_all(inverse, 'tr', split_axis=0, concat_axis=1, tiled=True)  47.5 us
    all_to_all x3, blocking collectives, copy_for_each(): lax.all_to_all(jnp.broadcast_to(x[None], (count, *x.shape)), axis, 0, 0,...  44.9 us
    another operation x12, other arithmetic  43.4 us
    ppermute x6, waiting for transfers between devices, shifted(): return lax.ppermute(value, axis, pairs)  26.4 us
    ppermute x6, starting transfers between devices, shifted(): return lax.ppermute(value, axis, pairs)  24.3 us
    dot_general x5, matrix products, forward_rows(): both_parts = jnp.dot(table, spectrum, preferred_element_type=jnp.float32)  22.7 us
    dot_general x16, matrix products, deposit(): lax.dot_general(weight_rows.astype(jnp.bfloat16), weight_cols.astype(jnp....  20.4 us
  transfers between devices with their start and end apart: 15, of which 10 were waited for; matrix products, arithmetic and copies ran while one was open for 6% of the time, Pallas kernels for 0%

commit v1 on v0

v1 whole, which is shorter than its diff:
```python
import functools
import math

import jax
import jax.numpy as jnp
import numpy as np
from jax import lax
from jax.experimental import pallas as pl
from jax.experimental.pallas import tpu as pltpu
from jax.sharding import PartitionSpec as P

SECTIONS = 4
GROUP = 4
LANES = 128
DRIFT = 0.5
MESH = pl.DeviceIdType.MESH


def row_tables(period):
    quarter = period // 4
    near = np.arange(quarter)
    forward, backward = [], []
    for residue in range(4):
        angle = 2.0 * np.pi / period * ((near[:, None] * (4 * near[None, :] + residue)) % period)
        forward.append(np.concatenate([np.cos(angle), np.sin(angle)], axis=1))
        backward.append(np.concatenate([np.cos(angle).T, np.sin(angle).T], axis=1))
    return np.stack(forward).astype(jnp.bfloat16), np.stack(backward).astype(jnp.bfloat16)


def column_tables(period):
    extent = period // 2
    count = extent // GROUP
    column = np.arange(extent)
    tables, slopes = [], []
    for rank in range(GROUP):
        twice = 2 * (GROUP * np.arange(count) + rank) + 1
        angle = np.pi / period * ((twice[:, None] * column[None, :]) % (2 * period))
        tables.append(np.concatenate([np.cos(angle), -np.sin(angle)], axis=0))
        slopes.append(np.repeat(np.sin(np.pi / period * twice)[:, None], LANES, axis=1))
    return np.stack(tables).astype(jnp.bfloat16), np.stack(slopes).astype(np.float32)


def dot(left, right):
    return lax.dot_general(left, right, (((1,), (0,)), ((), ())), preferred_element_type=jnp.float32)


def dot_t(left, right):
    return lax.dot_general(left, right, (((1,), (1,)), ((), ())), preferred_element_type=jnp.float32)


def kernel(
    sizes,
    cells_ref, offsets_ref, charges_ref, momenta_ref, green_ref, column_hbm, slope_hbm, forward_hbm, backward_hbm,
    out_ref,
    green_buf, column_buf, slope_buf, forward_buf, backward_buf, spectrum_re, spectrum_im,
    sums, charged, weight_rows, grid_spec, momenta_all, forward_src, forward_dst, kick_src, kick_dst, last_src, last_dst,
    load_sem, send_mom, recv_mom, send_fwd, recv_fwd, send_kick, recv_kick, send_last, recv_last,
):
    columns, planes, extent, particles = sizes
    period = 2 * extent
    quarter = period // 4
    count = extent // GROUP
    tiles = particles // LANES
    width = particles // planes
    bf16 = jnp.bfloat16

    c = lax.axis_index("cuts")
    t = lax.axis_index("tr")
    rank = lax.rem(t, GROUP)
    base = t - rank
    ahead = lax.rem(c + columns - 2, columns)
    behind = lax.rem(c + 2, columns)
    home = lax.rem(c + 2 * (SECTIONS - 1), columns)
    origin = lax.rem(c + columns - 2 * (SECTIONS - 1), columns)

    def member(step):
        return base + lax.rem(rank + step, GROUP)

    green_at = [pltpu.make_async_copy(green_ref.at[:, pl.ds(h * extent, extent)], green_buf.at[h], load_sem.at[h]) for h in range(2)]
    column_at = pltpu.make_async_copy(column_hbm.at[rank], column_buf, load_sem.at[2])
    slope_at = pltpu.make_async_copy(slope_hbm.at[rank], slope_buf, load_sem.at[3])
    forward_at = pltpu.make_async_copy(forward_hbm, forward_buf, load_sem.at[4])
    backward_at = pltpu.make_async_copy(backward_hbm, backward_buf, load_sem.at[5])
    for load in (column_at, green_at[0], green_at[1], forward_at, backward_at, slope_at):
        load.start()

    barrier = pltpu.get_barrier_semaphore()

    def greet(column, plane):
        pl.semaphore_signal(barrier, inc=1, device_id={"cuts": column, "tr": plane}, device_id_type=MESH)

    for step in range(1, planes):
        greet(c, lax.rem(t + step, planes))
    for step in range(planes):
        greet(ahead, lax.rem(t + step, planes))
        greet(behind, lax.rem(t + step, planes))
    for step in range(GROUP):
        greet(home, member(step))
        greet(origin, member(step))
    greeted = planes - 1 + 2 * planes + 2 * GROUP

    def packed(ref, lead):
        return jnp.concatenate([ref[lead + (slice(LANES * i, LANES * (i + 1)),)][None] for i in range(tiles)], axis=0)

    position = [
        [packed(cells_ref, (b, 0, d)).astype(jnp.float32) + packed(offsets_ref, (b, 0, d)) for d in range(2)] for b in range(2)
    ]
    charge = [packed(charges_ref, (b, 0)) for b in range(2)]
    momentum = [[None, None], [None, None]]

    def copy_to(source, target, send, receive, column, plane):
        return pltpu.make_async_remote_copy(
            src_ref=source, dst_ref=target, send_sem=send, recv_sem=receive,
            device_id={"cuts": column, "tr": plane}, device_id_type=MESH,
        )

    sends = []

    def forward_copy(section):
        return copy_to(forward_src.at[section], forward_dst.at[section], send_fwd.at[section], recv_fwd.at[section], ahead, t)

    def momenta_copy(b, step):
        column = c if b == 0 else ahead
        return copy_to(
            momenta_ref.at[b], momenta_all.at[b, step], send_mom.at[b, step], recv_mom.at[b, step], column, lax.rem(t + step, planes)
        )

    def kick_copy(section, b, step):
        column = c if b == 0 else ahead
        return copy_to(
            kick_src.at[section, b], kick_dst.at[section, b, step], send_kick.at[section, b, step], recv_kick.at[section, b, step],
            column, member(step),
        )

    def last_copy(b, step):
        column = c if b == 0 else home
        plane = member(step)
        return copy_to(
            last_src.at[b, (plane * width) // LANES], last_dst.at[b, step], send_last.at[b, step], recv_last.at[b, step], column, plane
        )

    def put_forward(section, parts):
        for i, part in enumerate(parts):
            forward_src[section, i] = part

    def hats(place, tile):
        nodes = lax.broadcasted_iota(jnp.int32, (extent, LANES), 0).astype(jnp.float32)
        distance = jnp.abs(nodes - place[tile : tile + 1, :])
        return jnp.maximum(1.0 - distance, 0.0).astype(bf16)

    def hat_pair(place, pair):
        return jnp.concatenate([hats(place, 2 * pair), hats(place, 2 * pair + 1)], axis=1)

    def column_sums(b):
        for pair in range(tiles // 2):
            span = slice(2 * LANES * pair, 2 * LANES * (pair + 1))
            found = dot(column_buf[...], hat_pair(position[b][1], pair))
            sums[b, :, span] = found
            heavy = jnp.concatenate([charge[b][2 * pair : 2 * pair + 1], charge[b][2 * pair + 1 : 2 * pair + 2]], axis=1)
            charged[b, :, span] = (found * heavy).astype(bf16)
            weight_rows[b, :, span] = hat_pair(position[b][0], pair)

    def column_spectrum(b):
        grid_spec[...] = dot_t(charged[b], weight_rows[b])

    def quarter_turns(re, im):
        if len(re) == 2:
            return [
                (re[0] + re[1], im[0] + im[1]),
                (re[0] + im[1], im[0] - re[1]),
                (re[0] - re[1], im[0] - im[1]),
                (re[0] - im[1], im[0] + re[1]),
            ]
        even_re, odd_re = re[0] + re[2], re[1] + re[3]
        even_im, odd_im = im[0] + im[2], im[1] + im[3]
        far_re, turn_re = re[0] - re[2], re[1] - re[3]
        far_im, turn_im = im[0] - im[2], im[1] - im[3]
        return [
            (even_re + odd_re, even_im + odd_im),
            (far_re + turn_im, far_im - turn_re),
            (even_re - odd_re, even_im - odd_im),
            (far_re - turn_im, far_im + turn_re),
        ]

    def to_rows(pair, residue):
        both = dot(jnp.concatenate([pair[0], pair[1]], axis=0).astype(bf16), forward_buf[residue])
        real = both[:count, :quarter] + both[count:, quarter:]
        imag = both[count:, :quarter] - both[:count, quarter:]
        return real, imag

    def kernel_spectrum():
        for load in green_at:
            load.wait()
        near = dot_t(column_buf[...], green_buf[0].astype(bf16))
        far = dot_t(column_buf[...], green_buf[1].astype(bf16))
        sign = (1 - 2 * lax.rem(rank, 2)).astype(jnp.float32)
        re = near[:count] - sign * far[count:]
        im = near[count:] + sign * far[:count]
        quarters = [slice(quarter * m, quarter * (m + 1)) for m in range(4)]
        turns = quarter_turns([re[:, q] for q in quarters], [im[:, q] for q in quarters])
        scale = 2.0 / (period * period)
        for residue in range(4):
            real, imag = to_rows(turns[residue], residue)
            spectrum_re[residue] = real * scale
            spectrum_im[residue] = imag * scale

    def field_spectra():
        halves = [slice(0, quarter), slice(quarter, extent)]
        turns = quarter_turns([grid_spec[:count, h] for h in halves], [grid_spec[count:, h] for h in halves])
        back = []
        for residue in range(4):
            x_re, x_im = to_rows(turns[residue], residue)
            k_re, k_im = spectrum_re[residue], spectrum_im[residue]
            z = jnp.concatenate([x_re * k_re - x_im * k_im, x_re * k_im + x_im * k_re], axis=0).astype(bf16)
            both = dot(z, backward_buf[residue])
            back.append((both[:count, :quarter] - both[count:, quarter:], both[count:, :quarter] + both[:count, quarter:]))
        (a_re, a_im), (b_re, b_im), (c_re, c_im), (d_re, d_im) = back
        even_re, even_im, odd_re, odd_im = a_re + c_re, a_im + c_im, b_re + d_re, b_im + d_im
        far_re, far_im, turn_re, turn_im = a_re - c_re, a_im - c_im, b_re - d_re, b_im - d_im
        v_re = jnp.concatenate([even_re + odd_re, far_re - turn_im], axis=1)
        v_im = jnp.concatenate([even_im + odd_im, far_im + turn_re], axis=1)
        v = jnp.concatenate([v_re, v_im], axis=0)
        along_rows = 0.5 * (pltpu.roll(v, 1, 1) - pltpu.roll(v, extent - 1, 1))
        slope = jnp.concatenate([slope_buf[...]] * (extent // LANES), axis=1)
        return jnp.concatenate([along_rows.astype(bf16), (slope * v_im).astype(bf16), (-slope * v_re).astype(bf16)], axis=0)

    def kicks_on(b, spectra):
        rows = [[], []]
        for pair in range(tiles // 2):
            span = slice(2 * LANES * pair, 2 * LANES * (pair + 1))
            reached = dot(spectra, weight_rows[b, :, span])
            own = sums[b, :, span]
            for d in range(2):
                terms = reached[2 * count * d : 2 * count * (d + 1)] * own
                total = jnp.sum(jnp.sum(terms.reshape(2 * count // 8, 8, 2 * LANES), axis=0), axis=0, keepdims=True)
                rows[d] += [total[:, :LANES], total[:, LANES:]]
        return [jnp.concatenate(rows[d], axis=0) for d in range(2)]

    def send_kicks(section, b, parts):
        own = jnp.concatenate(parts, axis=0).astype(bf16)
        kick_src[section, b] = own
        for step in range(1 if b == 0 else 0, GROUP):
            copy = kick_copy(section, b, step)
            copy.start()
            sends.append(copy)
        return own

    def whole_momenta(b):
        for step in range(1 if b == 0 else 0, planes):
            momenta_copy(b, step).wait_recv()
        if b == 0:
            momenta_all[0, 0] = momenta_ref[0]
        result = []
        for d in range(2):
            each = []
            for plane in range(planes):
                slot = lax.rem(t - plane + planes, planes)
                each.append(momenta_all[b, slot, 0, d][None])
            share = LANES // width
            rows = [each[i] if share == 1 else jnp.concatenate(each[share * i : share * (i + 1)], axis=1) for i in range(tiles)]
            result.append(jnp.concatenate(rows, axis=0))
        return result

    def arrive(section, b, own):
        if b == 0:
            if section == 0:
                momentum[0] = whole_momenta(0)
            old = [position[0][d] + DRIFT * momentum[0][d] for d in range(2)]
        else:
            forward_copy(section).wait_recv()
            old = [forward_dst[section, d] for d in range(2)]
            momentum[1] = whole_momenta(1) if section == 0 else [forward_dst[section, 2 + d] for d in range(2)]
            charge[1] = forward_dst[section, 4]
            if section == 0:
                old = [old[d] + DRIFT * momentum[1][d] for d in range(2)]
        total = own.astype(jnp.float32) if b == 0 else None
        for step in range(1 if b == 0 else 0, GROUP):
            kick_copy(section, b, step).wait_recv()
            part = kick_dst[section, b, step].astype(jnp.float32)
            total = part if total is None else total + part
        for d in range(2):
            kick = total[tiles * d : tiles * (d + 1)]
            momentum[b][d] = momentum[b][d] + kick
            position[b][d] = jnp.clip(old[d] + DRIFT * kick, 1.0, extent - 2.0 - 1.0 / 64.0)
        if b == 1 and section + 1 < SECTIONS - 1:
            put_forward(section + 1, [position[1][d] + DRIFT * momentum[1][d] for d in range(2)] + momentum[1] + [charge[1]])
            copy = forward_copy(section + 1)
            copy.start()
            sends.append(copy)

    def send_last_kicks(b, parts):
        for i in range(tiles):
            rows = [parts[d][i : i + 1] for d in range(2)]
            last_src[b, i] = jnp.concatenate(rows + [jnp.zeros((6, LANES), jnp.float32)], axis=0)
        for step in range(1 if b == 0 else 0, GROUP):
            copy = last_copy(b, step)
            copy.start()
            sends.append(copy)

    def own_lanes(tile):
        share = LANES // width
        if share == 1:
            return tile
        place = lax.rem(t, share)
        result = tile[:, :width]
        for i in range(1, share):
            result = jnp.where(place == i, tile[:, width * i : width * (i + 1)], result)
        return result

    put_forward(0, position[1] + [jnp.zeros_like(charge[1])] * 2 + [charge[1]])
    column_at.wait()
    own_kicks = [None, None]
    first = 1
    for section in range(SECTIONS):
        second = 1 - first
        if section > 0:
            arrive(section - 1, first, own_kicks[first])
        column_sums(first)
        column_spectrum(first)
        if section == 0:
            for load in (forward_at, backward_at, slope_at):
                load.wait()
            kernel_spectrum()
        spectra = field_spectra()
        if section > 0:
            arrive(section - 1, second, own_kicks[second])
        column_sums(second)
        if section == 0:
            pl.semaphore_wait(barrier, greeted)
            copies = [forward_copy(0)] + [momenta_copy(b, step) for b in range(2) for step in range(1 - b, planes)]
            for copy in copies:
                copy.start()
            sends += copies
        for source, target in ((first, second), (second, first)):
            if source == second:
                column_spectrum(second)
                spectra = field_spectra()
            parts = kicks_on(target, spectra)
            if section + 1 < SECTIONS:
                own_kicks[target] = send_kicks(section, target, parts)
            else:
                share = 1.0 / GROUP
                send_last_kicks(target, [parts[d] + share * momentum[target][d] for d in range(2)])
        first = second

    for b in (1, 0):
        total = last_src[0, (t * width) // LANES] if b == 0 else None
        for step in range(1 if b == 0 else 0, GROUP):
            last_copy(b, step).wait_recv()
            total = last_dst[b, step] if total is None else total + last_dst[b, step]
        out_ref[b, 0] = own_lanes(total[0:2])
    for copy in sends:
        copy.wait_send()


def per_device(mesh_shape, cells, offsets, charges, momenta, green):
    columns, planes = mesh_shape
    period = green.shape[0]
    extent = period // 2
    quarter = period // 4
    particles = cells.shape[-1]
    tiles = particles // LANES
    count = extent // GROUP
    forward, backward = row_tables(period)
    column, slope = column_tables(period)
    vmem = pl.BlockSpec(memory_space=pltpu.VMEM)
    anywhere = pl.BlockSpec(memory_space=pl.ANY)
    dma = pltpu.SemaphoreType.DMA
    f32, bf16 = jnp.float32, jnp.bfloat16
    return pl.pallas_call(
        functools.partial(kernel, (columns, planes, extent, particles)),
        out_shape=jax.ShapeDtypeStruct(momenta.shape, momenta.dtype),
        in_specs=[vmem] * 4 + [anywhere] * 5,
        out_specs=vmem,
        scratch_shapes=[
            pltpu.VMEM((2, period, extent), f32),
            pltpu.VMEM((2 * count, extent), bf16),
            pltpu.VMEM((count, LANES), f32),
            pltpu.VMEM((4, quarter, 2 * quarter), bf16),
            pltpu.VMEM((4, quarter, 2 * quarter), bf16),
            pltpu.VMEM((4, count, quarter), f32),
            pltpu.VMEM((4, count, quarter), f32),
            pltpu.VMEM((2, 2 * count, particles), f32),
            pltpu.VMEM((2, 2 * count, particles), bf16),
            pltpu.VMEM((2, extent, particles), bf16),
            pltpu.VMEM((2 * count, extent), f32),
            pltpu.VMEM((2, planes, *momenta.shape[1:]), f32),
            pltpu.VMEM((SECTIONS - 1, 5, tiles, LANES), f32),
            pltpu.VMEM((SECTIONS - 1, 5, tiles, LANES), f32),
            pltpu.VMEM((SECTIONS - 1, 2, 2 * tiles, LANES), bf16),
            pltpu.VMEM((SECTIONS - 1, 2, GROUP, 2 * tiles, LANES), bf16),
            pltpu.VMEM((2, tiles, 8, LANES), f32),
            pltpu.VMEM((2, GROUP, 8, LANES), f32),
            dma((6,)),
            dma((2, planes)),
            dma((2, planes)),
            dma((SECTIONS - 1,)),
            dma((SECTIONS - 1,)),
            dma((SECTIONS - 1, 2, GROUP)),
            dma((SECTIONS - 1, 2, GROUP)),
            dma((2, GROUP)),
            dma((2, GROUP)),
        ],
        compiler_params=pltpu.CompilerParams(collective_id=0, has_side_effects=True, vmem_limit_bytes=60 * 1024 * 1024),
    )(cells, offsets, charges, momenta, green, column, slope, forward, backward)


def solution(mesh):
    return jax.shard_map(
        functools.partial(per_device, (mesh.shape["cuts"], mesh.shape["tr"])),
        mesh=mesh,
        in_specs=(
            P(None, "cuts", None, None),
            P(None, "cuts", None, None),
            P(None, "cuts", None),
            P(None, "cuts", None, "tr"),
            P(),
        ),
        out_specs=P(None, "cuts", None, "tr"),
        check_vma=False,
    )
```

time: 443 us -> 52.6 us (0.12)
  the two profiles are of different devices: /device:TPU:6 before, /device:TPU:8 now
where the time goes in v1:
time: 52.6 us; the launch traced here: 52.4 us
  Pallas kernels  51.2 us (97%)
  local copies, waits for them, and re-layouts  1.26 us (2%)
    pallas_call x1, Pallas kernels, per_device(): pl.pallas_call(functools.partial(kernel, (columns, planes, extent, partic...  51.2 us
    unnamed x1, local copies, waits for them, and re-layouts  1.26 us

profile of v1, /device:TPU:8, one launch (start us, length us, event | category | flops | bytes accessed | tf_op | source)
XLA Modules:
  0.0 52.4 jit_solution(13956071568722648802)
XLA Ops:
  0.0 51.2 %shard_map.91 = f32[2,1,2,64]{3,2,1,0:T(2,128)} custom-call(s32[2,1,2,1024]{3,2,1,0:T(2,128)} %cells_ref.1, f32[2,1,2,1024]{3,2,1,0:T(2,128)} %offsets_ref.1, f32[2,1,1024]{2,1,0:T(1,128)} %charges_ref.1, f32[2,1,2,64]{3,2,1,0:T(2,128)} %momenta_ref.1, f32[1024,1024]{1,0:T(8,128)} %green_ref.1, bf16[4,256,512]{2,1,0:T(8,128)(2,1)} %constant.8.clone.column_hbm, ...), custom_call_target="tpu_custom_call" | custom-call | tf_op jit(solution)/shard_map/pallas_call | solution.py:370
  51.2 1.3 %copy.11 = f32[2,1,2,64]{3,2,1,0:T(2,128)} copy(f32[2,1,2,64]{3,2,1,0:T(2,128)} %shard_map.91) | data formatting | bytes 2048

commit v2 on v1

--- a/solution.py
+++ b/solution.py
@@ -16,28 +16,28 @@
 MESH = pl.DeviceIdType.MESH
 
 
+def turns(angle_steps, period):
+    angle = 2.0 * np.pi / period * (angle_steps % period)
+    return np.stack([np.cos(angle), np.sin(angle)], axis=-3).astype(np.float32)
+
+
 def row_tables(period):
-    quarter = period // 4
-    near = np.arange(quarter)
-    forward, backward = [], []
-    for residue in range(4):
-        angle = 2.0 * np.pi / period * ((near[:, None] * (4 * near[None, :] + residue)) % period)
-        forward.append(np.concatenate([np.cos(angle), np.sin(angle)], axis=1))
-        backward.append(np.concatenate([np.cos(angle).T, np.sin(angle).T], axis=1))
-    return np.stack(forward).astype(jnp.bfloat16), np.stack(backward).astype(jnp.bfloat16)
+    near = np.arange(period // 4)
+    coarse, fine = np.arange(period // 32), np.arange(8)
+    residue = np.arange(4)[:, None, None]
+    frequency = 4 * near[None, None, :] + residue
+    forward_coarse = turns(8 * coarse[None, :, None] * frequency, period)
+    forward_fine = turns(fine[None, :, None] * frequency, period)
+    backward_coarse = turns(32 * coarse[:, None] * near[None, :], period)
+    backward_fine = turns((4 * fine[None, :, None] + residue) * near[None, None, :], period)
+    return forward_coarse, forward_fine, backward_coarse, backward_fine
 
 
 def column_tables(period):
-    extent = period // 2
-    count = extent // GROUP
-    column = np.arange(extent)
-    tables, slopes = [], []
-    for rank in range(GROUP):
-        twice = 2 * (GROUP * np.arange(count) + rank) + 1
-        angle = np.pi / period * ((twice[:, None] * column[None, :]) % (2 * period))
-        tables.append(np.concatenate([np.cos(angle), -np.sin(angle)], axis=0))
-        slopes.append(np.repeat(np.sin(np.pi / period * twice)[:, None], LANES, axis=1))
-    return np.stack(tables).astype(jnp.bfloat16), np.stack(slopes).astype(np.float32)
+    column = np.arange(period // 2)
+    coarse = np.arange(period // 2 // GROUP // 8)
+    fine = 2 * (GROUP * np.arange(8)[None, :] + np.arange(GROUP)[:, None]) + 1
+    return turns(8 * GROUP * coarse[:, None] * column[None, :], period), turns(fine[:, :, None] * column, 2 * period)
 
 
 def dot(left, right):
@@ -50,12 +50,16 @@
 
 def kernel(
     sizes,
-    cells_ref, offsets_ref, charges_ref, momenta_ref, green_ref, column_hbm, slope_hbm, forward_hbm, backward_hbm,
-    out_ref,
-    green_buf, column_buf, slope_buf, forward_buf, backward_buf, spectrum_re, spectrum_im,
+    cells_ref, offsets_ref, charges_ref, momenta_ref, green_ref, column_hbm, column_fine_hbm, *row_hbm_and_rest,
+):
+    row_hbm = row_hbm_and_rest[:4]
+    (
+
+    out_ref, column_coarse, column_fine, *row_bufs_and_rest) = row_hbm_and_rest[4:]
+    row_bufs = row_bufs_and_rest[:4]
+    (green_buf, column_buf, slope_buf, forward_buf, backward_buf, spectrum_re, spectrum_im,
     sums, charged, weight_rows, grid_spec, momenta_all, forward_src, forward_dst, kick_src, kick_dst, last_src, last_dst,
-    load_sem, send_mom, recv_mom, send_fwd, recv_fwd, send_kick, recv_kick, send_last, recv_last,
-):
+    load_sem, send_mom, recv_mom, send_fwd, recv_fwd, send_kick, recv_kick, send_last, recv_last) = row_bufs_and_rest[4:]
     columns, planes, extent, particles = sizes
     period = 2 * extent
     quarter = period // 4
@@ -77,11 +81,12 @@
         return base + lax.rem(rank + step, GROUP)
 
     green_at = [pltpu.make_async_copy(green_ref.at[:, pl.ds(h * extent, extent)], green_buf.at[h], load_sem.at[h]) for h in range(2)]
-    column_at = pltpu.make_async_copy(column_hbm.at[rank], column_buf, load_sem.at[2])
-    slope_at = pltpu.make_async_copy(slope_hbm.at[rank], slope_buf, load_sem.at[3])
-    forward_at = pltpu.make_async_copy(forward_hbm, forward_buf, load_sem.at[4])
-    backward_at = pltpu.make_async_copy(backward_hbm, backward_buf, load_sem.at[5])
-    for load in (column_at, green_at[0], green_at[1], forward_at, backward_at, slope_at):
+    column_at = [
+        pltpu.make_async_copy(column_hbm, column_coarse, load_sem.at[2]),
+        pltpu.make_async_copy(column_fine_hbm.at[rank], column_fine, load_sem.at[3]),
+    ]
+    row_at = [pltpu.make_async_copy(row_hbm[i], row_bufs[i], load_sem.at[4 + i]) for i in range(4)]
+    for load in column_at + green_at + row_at:
         load.start()
 
     barrier = pltpu.get_barrier_semaphore()
@@ -91,13 +96,12 @@
 
     for step in range(1, planes):
         greet(c, lax.rem(t + step, planes))
-    for step in range(planes):
-        greet(ahead, lax.rem(t + step, planes))
-        greet(behind, lax.rem(t + step, planes))
     for step in range(GROUP):
+        greet(ahead, member(step))
+        greet(behind, member(step))
         greet(home, member(step))
         greet(origin, member(step))
-    greeted = planes - 1 + 2 * planes + 2 * GROUP
+    greeted = planes - 1 + 4 * GROUP
 
     def packed(ref, lead):
         return jnp.concatenate([ref[lead + (slice(LANES * i, LANES * (i + 1)),)][None] for i in range(tiles)], axis=0)
@@ -119,11 +123,8 @@
     def forward_copy(section):
         return copy_to(forward_src.at[section], forward_dst.at[section], send_fwd.at[section], recv_fwd.at[section], ahead, t)
 
-    def momenta_copy(b, step):
-        column = c if b == 0 else ahead
-        return copy_to(
-            momenta_ref.at[b], momenta_all.at[b, step], send_mom.at[b, step], recv_mom.at[b, step], column, lax.rem(t + step, planes)
-        )
+    def momenta_copy(step):
+        return copy_to(momenta_ref, momenta_all.at[step], send_mom.at[step], recv_mom.at[step], c, lax.rem(t + step, planes))
 
     def kick_copy(section, b, step):
         column = c if b == 0 else ahead
@@ -139,14 +140,60 @@
             last_src.at[b, (plane * width) // LANES], last_dst.at[b, step], send_last.at[b, step], recv_last.at[b, step], column, plane
         )
 
-    def put_forward(section, parts):
-        for i, part in enumerate(parts):
-            forward_src[section, i] = part
+    def turned(coarse_ref, fine_ref, lead, first):
+        far_cos, far_sin = coarse_ref[lead[0] + (0, slice(first, first + 1))], coarse_ref[lead[0] + (1, slice(first, first + 1))]
+        near_cos, near_sin = fine_ref[lead[1] + (0,)], fine_ref[lead[1] + (1,)]
+        return far_cos * near_cos - far_sin * near_sin, far_sin * near_cos + far_cos * near_sin
+
+    def fill_columns():
+        for load in column_at:
+            load.wait()
+        cosines, sines = [], []
+        for i in range(count // 8):
+            cosine, sine = turned(column_coarse, column_fine, ((), ()), i)
+            cosines.append(cosine.astype(bf16))
+            sines.append((-sine).astype(bf16))
+            slope_buf[8 * i : 8 * i + 8] = jnp.broadcast_to(sine[:, 1:2], (8, LANES))
+        for i in range(0, count // 8, 2):
+            column_buf[8 * i : 8 * i + 16] = jnp.concatenate(cosines[i : i + 2], axis=0)
+            column_buf[count + 8 * i : count + 8 * i + 16] = jnp.concatenate(sines[i : i + 2], axis=0)
+
+    def fill_rows():
+        for load in row_at:
+            load.wait()
+        forward_coarse, forward_fine, backward_coarse, backward_fine = row_bufs
+        for residue in range(4):
+            for i in range(0, quarter // 8, 2):
+                span = slice(8 * i, 8 * i + 16)
+                for buf, coarse, fine, lead in (
+                    (forward_buf, forward_coarse, forward_fine, ((residue,), (residue,))),
+                    (backward_buf, backward_coarse, backward_fine, ((), (residue,))),
+                ):
+                    one, two = turned(coarse, fine, lead, i), turned(coarse, fine, lead, i + 1)
+                    for part in range(2):
+                        both = jnp.concatenate([one[part], two[part]], axis=0).astype(bf16)
+                        buf[residue, span, quarter * part : quarter * (part + 1)] = both
+
+    side = 16
+    nodes = lax.broadcasted_iota(jnp.int32, (side, LANES), 0).astype(jnp.float32)
 
     def hats(place, tile):
-        nodes = lax.broadcasted_iota(jnp.int32, (extent, LANES), 0).astype(jnp.float32)
-        distance = jnp.abs(nodes - place[tile : tile + 1, :])
-        return jnp.maximum(1.0 - distance, 0.0).astype(bf16)
+        place = place[tile : tile + 1, :]
+        cell = jnp.floor(place)
+        high = place - cell
+        block = jnp.floor(cell * (1.0 / side))
+        node = cell - side * block
+        here = jnp.where(nodes == node, 1.0 - high, jnp.where(nodes == node + 1.0, high, 0.0)).astype(bf16)
+        following = jnp.where(nodes == node - (side - 1.0), high, 0.0).astype(bf16)
+        number = jnp.broadcast_to(block, (side, LANES)).astype(bf16)
+        none = jnp.zeros((side, LANES), bf16)
+        before, blocks = None, []
+        for k in range(extent // side):
+            mine = number == jnp.asarray(k, bf16)
+            rest = none if before is None else jnp.where(before, following, none)
+            blocks.append(jnp.where(mine, here, rest))
+            before = mine
+        return jnp.concatenate(blocks, axis=0)
 
     def hat_pair(place, pair):
         return jnp.concatenate([hats(place, 2 * pair), hats(place, 2 * pair + 1)], axis=1)
@@ -245,34 +292,36 @@
             sends.append(copy)
         return own
 
-    def whole_momenta(b):
-        for step in range(1 if b == 0 else 0, planes):
-            momenta_copy(b, step).wait_recv()
+    def whole_momenta():
+        momenta_all[0] = momenta_ref[...]
+        for step in range(1, planes):
+            momenta_copy(step).wait_recv()
+        share = LANES // width
+        for b in range(2):
+            for d in range(2):
+                each = [momenta_all[lax.rem(t - plane + planes, planes), b, 0, d][None] for plane in range(planes)]
+                rows = [jnp.concatenate(each[share * i : share * (i + 1)], axis=1) for i in range(tiles)]
+                momentum[b][d] = jnp.concatenate(rows, axis=0)
+
+    def pass_on(section):
+        parts = [position[1][d] + DRIFT * momentum[1][d] for d in range(2)] + momentum[1] + [charge[1]]
+        for i, part in enumerate(parts):
+            forward_src[section, i] = part
+        copy = forward_copy(section)
+        copy.start()
+        sends.append(copy)
+
+    def arrive(section, b, own):
+        if section == 0 and b == 0:
+            whole_momenta()
+            pass_on(0)
         if b == 0:
-            momenta_all[0, 0] = momenta_ref[0]
-        result = []
-        for d in range(2):
-            each = []
-            for plane in range(planes):
-                slot = lax.rem(t - plane + planes, planes)
-                each.append(momenta_all[b, slot, 0, d][None])
-            share = LANES // width
-            rows = [each[i] if share == 1 else jnp.concatenate(each[share * i : share * (i + 1)], axis=1) for i in range(tiles)]
-            result.append(jnp.concatenate(rows, axis=0))
-        return result
-
-    def arrive(section, b, own):
-        if b == 0:
-            if section == 0:
-                momentum[0] = whole_momenta(0)
             old = [position[0][d] + DRIFT * momentum[0][d] for d in range(2)]
         else:
             forward_copy(section).wait_recv()
             old = [forward_dst[section, d] for d in range(2)]
-            momentum[1] = whole_momenta(1) if section == 0 else [forward_dst[section, 2 + d] for d in range(2)]
+            momentum[1] = [forward_dst[section, 2 + d] for d in range(2)]
             charge[1] = forward_dst[section, 4]
-            if section == 0:
-                old = [old[d] + DRIFT * momentum[1][d] for d in range(2)]
         total = own.astype(jnp.float32) if b == 0 else None
         for step in range(1 if b == 0 else 0, GROUP):
             kick_copy(section, b, step).wait_recv()
@@ -283,10 +332,7 @@
             momentum[b][d] = momentum[b][d] + kick
             position[b][d] = jnp.clip(old[d] + DRIFT * kick, 1.0, extent - 2.0 - 1.0 / 64.0)
         if b == 1 and section + 1 < SECTIONS - 1:
-            put_forward(section + 1, [position[1][d] + DRIFT * momentum[1][d] for d in range(2)] + momentum[1] + [charge[1]])
-            copy = forward_copy(section + 1)
-            copy.start()
-            sends.append(copy)
+            pass_on(section + 1)
 
     def send_last_kicks(b, parts):
         for i in range(tiles):
@@ -307,8 +353,7 @@
             result = jnp.where(place == i, tile[:, width * i : width * (i + 1)], result)
         return result
 
-    put_forward(0, position[1] + [jnp.zeros_like(charge[1])] * 2 + [charge[1]])
-    column_at.wait()
+    fill_columns()
     own_kicks = [None, None]
     first = 1
     for section in range(SECTIONS):
@@ -318,8 +363,7 @@
         column_sums(first)
         column_spectrum(first)
         if section == 0:
-            for load in (forward_at, backward_at, slope_at):
-                load.wait()
+            fill_rows()
             kernel_spectrum()
         spectra = field_spectra()
         if section > 0:
@@ -327,7 +371,7 @@
         column_sums(second)
         if section == 0:
             pl.semaphore_wait(barrier, greeted)
-            copies = [forward_copy(0)] + [momenta_copy(b, step) for b in range(2) for step in range(1 - b, planes)]
+            copies = [momenta_copy(step) for step in range(1, planes)]
             for copy in copies:
                 copy.start()
             sends += copies
@@ -361,8 +405,7 @@
     particles = cells.shape[-1]
     tiles = particles // LANES
     count = extent // GROUP
-    forward, backward = row_tables(period)
-    column, slope = column_tables(period)
+    tables = column_tables(period) + row_tables(period)
     vmem = pl.BlockSpec(memory_space=pltpu.VMEM)
     anywhere = pl.BlockSpec(memory_space=pl.ANY)
     dma = pltpu.SemaphoreType.DMA
@@ -370,9 +413,12 @@
     return pl.pallas_call(
         functools.partial(kernel, (columns, planes, extent, particles)),
         out_shape=jax.ShapeDtypeStruct(momenta.shape, momenta.dtype),
-        in_specs=[vmem] * 4 + [anywhere] * 5,
+        in_specs=[vmem] * 4 + [anywhere] * 7,
         out_specs=vmem,
         scratch_shapes=[
+            pltpu.VMEM(tables[0].shape, f32),
+            pltpu.VMEM(tables[1].shape[1:], f32),
+            *[pltpu.VMEM(table.shape, f32) for table in tables[2:]],
             pltpu.VMEM((2, period, extent), f32),
             pltpu.VMEM((2 * count, extent), bf16),
             pltpu.VMEM((count, LANES), f32),
@@ -384,16 +430,16 @@
             pltpu.VMEM((2, 2 * count, particles), bf16),
             pltpu.VMEM((2, extent, particles), bf16),
             pltpu.VMEM((2 * count, extent), f32),
-            pltpu.VMEM((2, planes, *momenta.shape[1:]), f32),
+            pltpu.VMEM((planes, *momenta.shape), f32),
             pltpu.VMEM((SECTIONS - 1, 5, tiles, LANES), f32),
             pltpu.VMEM((SECTIONS - 1, 5, tiles, LANES), f32),
             pltpu.VMEM((SECTIONS - 1, 2, 2 * tiles, LANES), bf16),
             pltpu.VMEM((SECTIONS - 1, 2, GROUP, 2 * tiles, LANES), bf16),
             pltpu.VMEM((2, tiles, 8, LANES), f32),
             pltpu.VMEM((2, GROUP, 8, LANES), f32),
-            dma((6,)),
-            dma((2, planes)),
-            dma((2, planes)),
+            dma((8,)),
+            dma((planes,)),
+            dma((planes,)),
             dma((SECTIONS - 1,)),
             dma((SECTIONS - 1,)),
             dma((SECTIONS - 1, 2, GROUP)),
@@ -402,7 +448,7 @@
             dma((2, GROUP)),
         ],
         compiler_params=pltpu.CompilerParams(collective_id=0, has_side_effects=True, vmem_limit_bytes=60 * 1024 * 1024),
-    )(cells, offsets, charges, momenta, green, column, slope, forward, backward)
+    )(cells, offsets, charges, momenta, green, *tables)
 
 
 def solution(mesh):

time: 52.6 us -> 56.8 us (1.080)
  Pallas kernels: 51.2 us -> 55.3 us
    pallas_call x1, Pallas kernels: 51.2 us -> 55.3 us  [per_device(): pl.pallas_call(functools.partial(kernel, (columns, planes, extent, partic...]
where the time goes in v2:
time: 56.8 us; the launch traced here: 56.5 us
  Pallas kernels  55.3 us (97%)
  local copies, waits for them, and re-layouts  1.26 us (2%)
    pallas_call x1, Pallas kernels, per_device(): pl.pallas_call(functools.partial(kernel, (columns, planes, extent, partic...  55.3 us
    unnamed x1, local copies, waits for them, and re-layouts  1.26 us

profile of v2, /device:TPU:8, one launch (start us, length us, event | category | flops | bytes accessed | tf_op | source)
XLA Modules:
  0.0 56.5 jit_solution(5523813160486843537)
XLA Ops:
  0.0 55.3 %shard_map.109 = f32[2,1,2,64]{3,2,1,0:T(2,128)} custom-call(s32[2,1,2,1024]{3,2,1,0:T(2,128)} %cells_ref.1, f32[2,1,2,1024]{3,2,1,0:T(2,128)} %offsets_ref.1, f32[2,1,1024]{2,1,0:T(1,128)} %charges_ref.1, f32[2,1,2,64]{3,2,1,0:T(2,128)} %momenta_ref.1, f32[1024,1024]{1,0:T(8,128)} %green_ref.1, f32[2,16,512]{2,1,0:T(8,128)} %constant.12.clone.column_hbm, ...), custom_call_target="tpu_custom_call" | custom-call | tf_op jit(solution)/shard_map/pallas_call | solution.py:413
  55.3 1.3 %copy.13 = f32[2,1,2,64]{3,2,1,0:T(2,128)} copy(f32[2,1,2,64]{3,2,1,0:T(2,128)} %shard_map.109) | data formatting | bytes 2048

commit v3 on v2

--- a/solution.py
+++ b/solution.py
@@ -59,7 +59,7 @@
     row_bufs = row_bufs_and_rest[:4]
     (green_buf, column_buf, slope_buf, forward_buf, backward_buf, spectrum_re, spectrum_im,
     sums, charged, weight_rows, grid_spec, momenta_all, forward_src, forward_dst, kick_src, kick_dst, last_src, last_dst,
-    load_sem, send_mom, recv_mom, send_fwd, recv_fwd, send_kick, recv_kick, send_last, recv_last) = row_bufs_and_rest[4:]
+    load_sem, send_mom, recv_mom, send_relay, recv_relay, send_fwd, recv_fwd, send_kick, recv_kick, send_last, recv_last) = row_bufs_and_rest[4:]
     columns, planes, extent, particles = sizes
     period = 2 * extent
     quarter = period // 4
@@ -94,14 +94,18 @@
     def greet(column, plane):
         pl.semaphore_signal(barrier, inc=1, device_id={"cuts": column, "tr": plane}, device_id_type=MESH)
 
-    for step in range(1, planes):
-        greet(c, lax.rem(t + step, planes))
+    half = planes // 4
+    reach = max(half, GROUP - 1)
+    for step in range(-reach, reach + 1):
+        plane = lax.rem(t + step + planes, planes)
+        if step != 0:
+            greet(c, plane)
+        greet(ahead, plane)
+        greet(behind, plane)
     for step in range(GROUP):
-        greet(ahead, member(step))
-        greet(behind, member(step))
         greet(home, member(step))
         greet(origin, member(step))
-    greeted = planes - 1 + 4 * GROUP
+    greeted = 3 * (2 * reach + 1) - 1 + 2 * GROUP
 
     def packed(ref, lead):
         return jnp.concatenate([ref[lead + (slice(LANES * i, LANES * (i + 1)),)][None] for i in range(tiles)], axis=0)
@@ -123,8 +127,22 @@
     def forward_copy(section):
         return copy_to(forward_src.at[section], forward_dst.at[section], send_fwd.at[section], recv_fwd.at[section], ahead, t)
 
-    def momenta_copy(step):
-        return copy_to(momenta_ref, momenta_all.at[step], send_mom.at[step], recv_mom.at[step], c, lax.rem(t + step, planes))
+    def momenta_copy(b, step):
+        slot = 2 * half - step
+        return copy_to(
+            momenta_ref.at[b], momenta_all.at[b, slot], send_mom.at[b, slot], recv_mom.at[b, slot],
+            c if b == 0 else ahead, lax.rem(t + step + planes, planes),
+        )
+
+    near_steps = [[step for step in range(-half, half + 1) if b == 1 or step != 0] for b in range(2)]
+
+    def relay_copy(b, up):
+        first, last, target = (half, 2 * half, 0) if up else (2 * half + 1, 3 * half, 3 * half + 1)
+        return copy_to(
+            momenta_all.at[b, first:last], momenta_all.at[b, target : target + last - first],
+            send_relay.at[b, int(up)], recv_relay.at[b, int(up)],
+            c, lax.rem(t + (half if up else planes - half), planes),
+        )
 
     def kick_copy(section, b, step):
         column = c if b == 0 else ahead
@@ -292,19 +310,28 @@
             sends.append(copy)
         return own
 
-    def whole_momenta():
-        momenta_all[0] = momenta_ref[...]
-        for step in range(1, planes):
-            momenta_copy(step).wait_recv()
+    def relay_momenta():
+        momenta_all[0, 2 * half] = momenta_ref[0]
+        for b in range(2):
+            for step in near_steps[b]:
+                momenta_copy(b, step).wait_recv()
+            for up in (True, False):
+                copy = relay_copy(b, up)
+                copy.start()
+                sends.append(copy)
+
+    def whole_momenta(b):
+        for up in (True, False):
+            relay_copy(b, up).wait_recv()
         share = LANES // width
-        for b in range(2):
-            for d in range(2):
-                each = [momenta_all[lax.rem(t - plane + planes, planes), b, 0, d][None] for plane in range(planes)]
-                rows = [jnp.concatenate(each[share * i : share * (i + 1)], axis=1) for i in range(tiles)]
-                momentum[b][d] = jnp.concatenate(rows, axis=0)
-
-    def pass_on(section):
-        parts = [position[1][d] + DRIFT * momentum[1][d] for d in range(2)] + momentum[1] + [charge[1]]
+        result = []
+        for d in range(2):
+            each = [momenta_all[b, lax.rem(plane - t + 2 * half + planes, planes), 0, d][None] for plane in range(planes)]
+            rows = [jnp.concatenate(each[share * i : share * (i + 1)], axis=1) for i in range(tiles)]
+            result.append(jnp.concatenate(rows, axis=0))
+        return result
+
+    def pass_on(section, parts):
         for i, part in enumerate(parts):
             forward_src[section, i] = part
         copy = forward_copy(section)
@@ -312,16 +339,19 @@
         sends.append(copy)
 
     def arrive(section, b, own):
-        if section == 0 and b == 0:
-            whole_momenta()
-            pass_on(0)
         if b == 0:
+            if section == 0:
+                momentum[0] = whole_momenta(0)
             old = [position[0][d] + DRIFT * momentum[0][d] for d in range(2)]
         else:
             forward_copy(section).wait_recv()
             old = [forward_dst[section, d] for d in range(2)]
-            momentum[1] = [forward_dst[section, 2 + d] for d in range(2)]
             charge[1] = forward_dst[section, 4]
+            if section == 0:
+                momentum[1] = whole_momenta(1)
+                old = [old[d] + DRIFT * momentum[1][d] for d in range(2)]
+            else:
+                momentum[1] = [forward_dst[section, 2 + d] for d in range(2)]
         total = own.astype(jnp.float32) if b == 0 else None
         for step in range(1 if b == 0 else 0, GROUP):
             kick_copy(section, b, step).wait_recv()
@@ -332,7 +362,7 @@
             momentum[b][d] = momentum[b][d] + kick
             position[b][d] = jnp.clip(old[d] + DRIFT * kick, 1.0, extent - 2.0 - 1.0 / 64.0)
         if b == 1 and section + 1 < SECTIONS - 1:
-            pass_on(section + 1)
+            pass_on(section + 1, [position[1][d] + DRIFT * momentum[1][d] for d in range(2)] + momentum[1] + [charge[1]])
 
     def send_last_kicks(b, parts):
         for i in range(tiles):
@@ -371,7 +401,8 @@
         column_sums(second)
         if section == 0:
             pl.semaphore_wait(barrier, greeted)
-            copies = [momenta_copy(step) for step in range(1, planes)]
+            pass_on(0, position[1] + [jnp.zeros_like(charge[1])] * 2 + [charge[1]])
+            copies = [momenta_copy(b, step) for b in range(2) for step in near_steps[b]]
             for copy in copies:
                 copy.start()
             sends += copies
@@ -385,6 +416,8 @@
             else:
                 share = 1.0 / GROUP
                 send_last_kicks(target, [parts[d] + share * momentum[target][d] for d in range(2)])
+        if section == 0:
+            relay_momenta()
         first = second
 
     for b in (1, 0):
@@ -430,7 +463,7 @@
             pltpu.VMEM((2, 2 * count, particles), bf16),
             pltpu.VMEM((2, extent, particles), bf16),
             pltpu.VMEM((2 * count, extent), f32),
-            pltpu.VMEM((planes, *momenta.shape), f32),
+            pltpu.VMEM((2, planes, *momenta.shape[1:]), f32),
             pltpu.VMEM((SECTIONS - 1, 5, tiles, LANES), f32),
             pltpu.VMEM((SECTIONS - 1, 5, tiles, LANES), f32),
             pltpu.VMEM((SECTIONS - 1, 2, 2 * tiles, LANES), bf16),
@@ -438,8 +471,10 @@
             pltpu.VMEM((2, tiles, 8, LANES), f32),
             pltpu.VMEM((2, GROUP, 8, LANES), f32),
             dma((8,)),
-            dma((planes,)),
-            dma((planes,)),
+            dma((2, planes)),
+            dma((2, planes)),
+            dma((2, 2)),
+            dma((2, 2)),
             dma((SECTIONS - 1,)),
             dma((SECTIONS - 1,)),
             dma((SECTIONS - 1, 2, GROUP)),

time: 56.8 us -> 58.3 us (1.026)
  the two profiles are of different devices: /device:TPU:8 before, /device:TPU:16 now
where the time goes in v3:
time: 58.3 us; the launch traced here: 58 us
  Pallas kernels  56.8 us (97%)
  local copies, waits for them, and re-layouts  1.26 us (2%)
    pallas_call x1, Pallas kernels, per_device(): pl.pallas_call(functools.partial(kernel, (columns, planes, extent, partic...  56.8 us
    unnamed x1, local copies, waits for them, and re-layouts  1.26 us

profile of v3, /device:TPU:16, one launch (start us, length us, event | category | flops | bytes accessed | tf_op | source)
XLA Modules:
  0.0 58.0 jit_solution(17866782909795305947)
XLA Ops:
  0.0 56.8 %shard_map.109 = f32[2,1,2,64]{3,2,1,0:T(2,128)} custom-call(s32[2,1,2,1024]{3,2,1,0:T(2,128)} %cells_ref.1, f32[2,1,2,1024]{3,2,1,0:T(2,128)} %offsets_ref.1, f32[2,1,1024]{2,1,0:T(1,128)} %charges_ref.1, f32[2,1,2,64]{3,2,1,0:T(2,128)} %momenta_ref.1, f32[1024,1024]{1,0:T(8,128)} %green_ref.1, f32[2,16,512]{2,1,0:T(8,128)} %constant.12.clone.column_hbm, ...), custom_call_target="tpu_custom_call" | custom-call | tf_op jit(solution)/shard_map/pallas_call | solution.py:446
  56.8 1.3 %copy.13 = f32[2,1,2,64]{3,2,1,0:T(2,128)} copy(f32[2,1,2,64]{3,2,1,0:T(2,128)} %shard_map.109) | data formatting | bytes 2048

commit v4 on v3

--- a/solution.py
+++ b/solution.py
@@ -58,8 +58,8 @@
     out_ref, column_coarse, column_fine, *row_bufs_and_rest) = row_hbm_and_rest[4:]
     row_bufs = row_bufs_and_rest[:4]
     (green_buf, column_buf, slope_buf, forward_buf, backward_buf, spectrum_re, spectrum_im,
-    sums, charged, weight_rows, grid_spec, momenta_all, forward_src, forward_dst, kick_src, kick_dst, last_src, last_dst,
-    load_sem, send_mom, recv_mom, send_relay, recv_relay, send_fwd, recv_fwd, send_kick, recv_kick, send_last, recv_last) = row_bufs_and_rest[4:]
+    sums, charged, weight_rows, grid_spec, turned_spec, product, scaled, returned, fields, near, far, momenta_all, forward_src, forward_dst, kick_src, kick_dst, last_src, last_dst,
+    load_sem, send_mom, recv_mom, send_fwd, recv_fwd, send_kick, recv_kick, send_last, recv_last) = row_bufs_and_rest[4:]
     columns, planes, extent, particles = sizes
     period = 2 * extent
     quarter = period // 4
@@ -94,18 +94,15 @@
     def greet(column, plane):
         pl.semaphore_signal(barrier, inc=1, device_id={"cuts": column, "tr": plane}, device_id_type=MESH)
 
-    half = planes // 4
-    reach = max(half, GROUP - 1)
-    for step in range(-reach, reach + 1):
-        plane = lax.rem(t + step + planes, planes)
-        if step != 0:
-            greet(c, plane)
-        greet(ahead, plane)
-        greet(behind, plane)
+    for step in range(1, planes):
+        greet(c, lax.rem(t + step, planes))
+    for step in range(planes):
+        greet(ahead, lax.rem(t + step, planes))
+        greet(behind, lax.rem(t + step, planes))
     for step in range(GROUP):
         greet(home, member(step))
         greet(origin, member(step))
-    greeted = 3 * (2 * reach + 1) - 1 + 2 * GROUP
+    greeted = planes - 1 + 2 * planes + 2 * GROUP
 
     def packed(ref, lead):
         return jnp.concatenate([ref[lead + (slice(LANES * i, LANES * (i + 1)),)][None] for i in range(tiles)], axis=0)
@@ -128,20 +125,9 @@
         return copy_to(forward_src.at[section], forward_dst.at[section], send_fwd.at[section], recv_fwd.at[section], ahead, t)
 
     def momenta_copy(b, step):
-        slot = 2 * half - step
+        column = c if b == 0 else ahead
         return copy_to(
-            momenta_ref.at[b], momenta_all.at[b, slot], send_mom.at[b, slot], recv_mom.at[b, slot],
-            c if b == 0 else ahead, lax.rem(t + step + planes, planes),
-        )
-
-    near_steps = [[step for step in range(-half, half + 1) if b == 1 or step != 0] for b in range(2)]
-
-    def relay_copy(b, up):
-        first, last, target = (half, 2 * half, 0) if up else (2 * half + 1, 3 * half, 3 * half + 1)
-        return copy_to(
-            momenta_all.at[b, first:last], momenta_all.at[b, target : target + last - first],
-            send_relay.at[b, int(up)], recv_relay.at[b, int(up)],
-            c, lax.rem(t + (half if up else planes - half), planes),
+            momenta_ref.at[b], momenta_all.at[b, step], send_mom.at[b, step], recv_mom.at[b, step], column, lax.rem(t + step, planes)
         )
 
     def kick_copy(section, b, step):
@@ -228,66 +214,104 @@
     def column_spectrum(b):
         grid_spec[...] = dot_t(charged[b], weight_rows[b])
 
-    def quarter_turns(re, im):
-        if len(re) == 2:
-            return [
-                (re[0] + re[1], im[0] + im[1]),
-                (re[0] + im[1], im[0] - re[1]),
-                (re[0] - re[1], im[0] - im[1]),
-                (re[0] - im[1], im[0] + re[1]),
-            ]
-        even_re, odd_re = re[0] + re[2], re[1] + re[3]
-        even_im, odd_im = im[0] + im[2], im[1] + im[3]
-        far_re, turn_re = re[0] - re[2], re[1] - re[3]
-        far_im, turn_im = im[0] - im[2], im[1] - im[3]
-        return [
-            (even_re + odd_re, even_im + odd_im),
-            (far_re + turn_im, far_im - turn_re),
-            (even_re - odd_re, even_im - odd_im),
-            (far_re - turn_im, far_im + turn_re),
-        ]
-
-    def to_rows(pair, residue):
-        both = dot(jnp.concatenate([pair[0], pair[1]], axis=0).astype(bf16), forward_buf[residue])
-        real = both[:count, :quarter] + both[count:, quarter:]
-        imag = both[count:, :quarter] - both[:count, quarter:]
+    side_rows = 16
+    row_blocks = [slice(side_rows * i, side_rows * (i + 1)) for i in range(count // side_rows)]
+
+    def imag_rows(rows):
+        return slice(count + rows.start, count + rows.stop)
+
+    def to_rows(residue):
+        product[residue] = dot(turned_spec[residue], forward_buf[residue])
+
+    def row_spectrum(residue, rows):
+        below = imag_rows(rows)
+        real = product[residue, rows, :quarter] + product[residue, below, quarter:]
+        imag = product[residue, below, :quarter] - product[residue, rows, quarter:]
         return real, imag
 
     def kernel_spectrum():
         for load in green_at:
             load.wait()
-        near = dot_t(column_buf[...], green_buf[0].astype(bf16))
-        far = dot_t(column_buf[...], green_buf[1].astype(bf16))
+        near[...] = dot_t(column_buf[...], green_buf[0].astype(bf16))
+        far[...] = dot_t(column_buf[...], green_buf[1].astype(bf16))
         sign = (1 - 2 * lax.rem(rank, 2)).astype(jnp.float32)
-        re = near[:count] - sign * far[count:]
-        im = near[count:] + sign * far[:count]
-        quarters = [slice(quarter * m, quarter * (m + 1)) for m in range(4)]
-        turns = quarter_turns([re[:, q] for q in quarters], [im[:, q] for q in quarters])
+        for rows in row_blocks:
+            below = imag_rows(rows)
+            re = [near[rows, quarter * m : quarter * (m + 1)] - sign * far[below, quarter * m : quarter * (m + 1)] for m in range(4)]
+            im = [near[below, quarter * m : quarter * (m + 1)] + sign * far[rows, quarter * m : quarter * (m + 1)] for m in range(4)]
+            even_re, odd_re, even_im, odd_im = re[0] + re[2], re[1] + re[3], im[0] + im[2], im[1] + im[3]
+            far_re, turn_re, far_im, turn_im = re[0] - re[2], re[1] - re[3], im[0] - im[2], im[1] - im[3]
+            put_turned(
+                rows,
+                (
+                    (even_re + odd_re, even_im + odd_im),
+                    (far_re + turn_im, far_im - turn_re),
+                    (even_re - odd_re, even_im - odd_im),
+                    (far_re - turn_im, far_im + turn_re),
+                ),
+            )
         scale = 2.0 / (period * period)
         for residue in range(4):
-            real, imag = to_rows(turns[residue], residue)
-            spectrum_re[residue] = real * scale
-            spectrum_im[residue] = imag * scale
+            to_rows(residue)
+        for residue in range(4):
+            for rows in row_blocks:
+                real, imag = row_spectrum(residue, rows)
+                spectrum_re[residue, rows] = real * scale
+                spectrum_im[residue, rows] = imag * scale
+
+    def put_turned(rows, turns_of):
+        for residue, (re, im) in enumerate(turns_of):
+            turned_spec[residue, rows] = re.astype(bf16)
+            turned_spec[residue, imag_rows(rows)] = im.astype(bf16)
 
     def field_spectra():
-        halves = [slice(0, quarter), slice(quarter, extent)]
-        turns = quarter_turns([grid_spec[:count, h] for h in halves], [grid_spec[count:, h] for h in halves])
-        back = []
+        for rows in row_blocks:
+            below = imag_rows(rows)
+            re = grid_spec[rows, :quarter], grid_spec[rows, quarter:]
+            im = grid_spec[below, :quarter], grid_spec[below, quarter:]
+            put_turned(
+                rows,
+                (
+                    (re[0] + re[1], im[0] + im[1]),
+                    (re[0] + im[1], im[0] - re[1]),
+                    (re[0] - re[1], im[0] - im[1]),
+                    (re[0] - im[1], im[0] + re[1]),
+                ),
+            )
+        to_rows(0)
         for residue in range(4):
-            x_re, x_im = to_rows(turns[residue], residue)
-            k_re, k_im = spectrum_re[residue], spectrum_im[residue]
-            z = jnp.concatenate([x_re * k_re - x_im * k_im, x_re * k_im + x_im * k_re], axis=0).astype(bf16)
-            both = dot(z, backward_buf[residue])
-            back.append((both[:count, :quarter] - both[count:, quarter:], both[count:, :quarter] + both[:count, quarter:]))
-        (a_re, a_im), (b_re, b_im), (c_re, c_im), (d_re, d_im) = back
-        even_re, even_im, odd_re, odd_im = a_re + c_re, a_im + c_im, b_re + d_re, b_im + d_im
-        far_re, far_im, turn_re, turn_im = a_re - c_re, a_im - c_im, b_re - d_re, b_im - d_im
-        v_re = jnp.concatenate([even_re + odd_re, far_re - turn_im], axis=1)
-        v_im = jnp.concatenate([even_im + odd_im, far_im + turn_re], axis=1)
-        v = jnp.concatenate([v_re, v_im], axis=0)
-        along_rows = 0.5 * (pltpu.roll(v, 1, 1) - pltpu.roll(v, extent - 1, 1))
-        slope = jnp.concatenate([slope_buf[...]] * (extent // LANES), axis=1)
-        return jnp.concatenate([along_rows.astype(bf16), (slope * v_im).astype(bf16), (-slope * v_re).astype(bf16)], axis=0)
+            if residue + 1 < 4:
+                to_rows(residue + 1)
+            for rows in row_blocks:
+                x_re, x_im = row_spectrum(residue, rows)
+                k_re, k_im = spectrum_re[residue, rows], spectrum_im[residue, rows]
+                scaled[residue, rows] = (x_re * k_re - x_im * k_im).astype(bf16)
+                scaled[residue, imag_rows(rows)] = (x_re * k_im + x_im * k_re).astype(bf16)
+            returned[residue] = dot(scaled[residue], backward_buf[residue])
+        for rows in row_blocks:
+            below = imag_rows(rows)
+            for part in range(quarter // LANES):
+                near_lanes = slice(LANES * part, LANES * (part + 1))
+                far_lanes = slice(quarter + LANES * part, quarter + LANES * (part + 1))
+                (a_re, a_im), (b_re, b_im), (c_re, c_im), (d_re, d_im) = [
+                    (
+                        returned[j, rows, near_lanes] - returned[j, below, far_lanes],
+                        returned[j, below, near_lanes] + returned[j, rows, far_lanes],
+                    )
+                    for j in range(4)
+                ]
+                grid_spec[rows, near_lanes] = (a_re + c_re) + (b_re + d_re)
+                grid_spec[below, near_lanes] = (a_im + c_im) + (b_im + d_im)
+                grid_spec[rows, far_lanes] = (a_re - c_re) - (b_im - d_im)
+                grid_spec[below, far_lanes] = (a_im - c_im) + (b_re - d_re)
+        for rows in row_blocks:
+            below = imag_rows(rows)
+            slope = jnp.concatenate([slope_buf[rows]] * (extent // LANES), axis=1)
+            for lines, twin, factor in ((rows, below, -slope), (below, rows, slope)):
+                v = grid_spec[lines]
+                fields[lines] = (0.5 * (pltpu.roll(v, 1, 1) - pltpu.roll(v, extent - 1, 1))).astype(bf16)
+                fields[slice(2 * count + twin.start, 2 * count + twin.stop)] = (factor * v).astype(bf16)
+        return fields[...]
 
     def kicks_on(b, spectra):
         rows = [[], []]
@@ -310,24 +334,19 @@
             sends.append(copy)
         return own
 
-    def relay_momenta():
-        momenta_all[0, 2 * half] = momenta_ref[0]
-        for b in range(2):
-            for step in near_steps[b]:
-                momenta_copy(b, step).wait_recv()
-            for up in (True, False):
-                copy = relay_copy(b, up)
-                copy.start()
-                sends.append(copy)
-
     def whole_momenta(b):
-        for up in (True, False):
-            relay_copy(b, up).wait_recv()
-        share = LANES // width
+        for step in range(1 if b == 0 else 0, planes):
+            momenta_copy(b, step).wait_recv()
+        if b == 0:
+            momenta_all[0, 0] = momenta_ref[0]
         result = []
         for d in range(2):
-            each = [momenta_all[b, lax.rem(plane - t + 2 * half + planes, planes), 0, d][None] for plane in range(planes)]
-            rows = [jnp.concatenate(each[share * i : share * (i + 1)], axis=1) for i in range(tiles)]
+            each = []
+            for plane in range(planes):
+                slot = lax.rem(t - plane + planes, planes)
+                each.append(momenta_all[b, slot, 0, d][None])
+            share = LANES // width
+            rows = [each[i] if share == 1 else jnp.concatenate(each[share * i : share * (i + 1)], axis=1) for i in range(tiles)]
             result.append(jnp.concatenate(rows, axis=0))
         return result
 
@@ -399,25 +418,23 @@
         if section > 0:
             arrive(section - 1, second, own_kicks[second])
         column_sums(second)
-        if section == 0:
-            pl.semaphore_wait(barrier, greeted)
-            pass_on(0, position[1] + [jnp.zeros_like(charge[1])] * 2 + [charge[1]])
-            copies = [momenta_copy(b, step) for b in range(2) for step in near_steps[b]]
-            for copy in copies:
-                copy.start()
-            sends += copies
         for source, target in ((first, second), (second, first)):
             if source == second:
                 column_spectrum(second)
                 spectra = field_spectra()
             parts = kicks_on(target, spectra)
+            if section == 0 and source == first:
+                pl.semaphore_wait(barrier, greeted)
+                copies = [momenta_copy(b, step) for b in range(2) for step in range(1 - b, planes)]
+                for copy in copies:
+                    copy.start()
+                sends += copies
+                pass_on(0, position[1] + [jnp.zeros_like(charge[1])] * 2 + [charge[1]])
             if section + 1 < SECTIONS:
                 own_kicks[target] = send_kicks(section, target, parts)
             else:
                 share = 1.0 / GROUP
                 send_last_kicks(target, [parts[d] + share * momentum[target][d] for d in range(2)])
-        if section == 0:
-            relay_momenta()
         first = second
 
     for b in (1, 0):
@@ -463,6 +480,13 @@
             pltpu.VMEM((2, 2 * count, particles), bf16),
             pltpu.VMEM((2, extent, particles), bf16),
             pltpu.VMEM((2 * count, extent), f32),
+            pltpu.VMEM((4, 2 * count, quarter), bf16),
+            pltpu.VMEM((4, 2 * count, 2 * quarter), f32),
+            pltpu.VMEM((4, 2 * count, quarter), bf16),
+            pltpu.VMEM((4, 2 * count, 2 * quarter), f32),
+            pltpu.VMEM((4 * count, extent), bf16),
+            pltpu.VMEM((2 * count, period), f32),
+            pltpu.VMEM((2 * count, period), f32),
             pltpu.VMEM((2, planes, *momenta.shape[1:]), f32),
             pltpu.VMEM((SECTIONS - 1, 5, tiles, LANES), f32),
             pltpu.VMEM((SECTIONS - 1, 5, tiles, LANES), f32),
@@ -473,8 +497,6 @@
             dma((8,)),
             dma((2, planes)),
             dma((2, planes)),
-            dma((2, 2)),
-            dma((2, 2)),
             dma((SECTIONS - 1,)),
             dma((SECTIONS - 1,)),
             dma((SECTIONS - 1, 2, GROUP)),

time: 58.3 us -> 57.3 us (0.983)
  Pallas kernels: 56.8 us -> 55.8 us
    pallas_call x1, Pallas kernels: 56.8 us -> 55.8 us  [per_device(): pl.pallas_call(functools.partial(kernel, (columns, planes, extent, partic...]
where the time goes in v4:
time: 57.3 us; the launch traced here: 57.1 us
  Pallas kernels  55.8 us (97%)
  local copies, waits for them, and re-layouts  1.26 us (2%)
    pallas_call x1, Pallas kernels, per_device(): pl.pallas_call(functools.partial(kernel, (columns, planes, extent, partic...  55.8 us
    unnamed x1, local copies, waits for them, and re-layouts  1.26 us

profile of v4, /device:TPU:16, one launch (start us, length us, event | category | flops | bytes accessed | tf_op | source)
XLA Modules:
  0.0 57.1 jit_solution(3253985528079856769)
XLA Ops:
  0.0 55.8 %shard_map.109 = f32[2,1,2,64]{3,2,1,0:T(2,128)} custom-call(s32[2,1,2,1024]{3,2,1,0:T(2,128)} %cells_ref.1, f32[2,1,2,1024]{3,2,1,0:T(2,128)} %offsets_ref.1, f32[2,1,1024]{2,1,0:T(1,128)} %charges_ref.1, f32[2,1,2,64]{3,2,1,0:T(2,128)} %momenta_ref.1, f32[1024,1024]{1,0:T(8,128)} %green_ref.1, f32[2,16,512]{2,1,0:T(8,128)} %constant.12.clone.column_hbm, ...), custom_call_target="tpu_custom_call" | custom-call | tf_op jit(solution)/shard_map/pallas_call | solution.py:463
  55.8 1.3 %copy.13 = f32[2,1,2,64]{3,2,1,0:T(2,128)} copy(f32[2,1,2,64]{3,2,1,0:T(2,128)} %shard_map.109) | data formatting | bytes 2048

commit v5 on v4

--- a/solution.py
+++ b/solution.py
@@ -59,7 +59,7 @@
     row_bufs = row_bufs_and_rest[:4]
     (green_buf, column_buf, slope_buf, forward_buf, backward_buf, spectrum_re, spectrum_im,
     sums, charged, weight_rows, grid_spec, turned_spec, product, scaled, returned, fields, near, far, momenta_all, forward_src, forward_dst, kick_src, kick_dst, last_src, last_dst,
-    load_sem, send_mom, recv_mom, send_fwd, recv_fwd, send_kick, recv_kick, send_last, recv_last) = row_bufs_and_rest[4:]
+    load_sem, fence_sem, send_mom, recv_mom, send_fwd, recv_fwd, send_kick, recv_kick, send_last, recv_last) = row_bufs_and_rest[4:]
     columns, planes, extent, particles = sizes
     period = 2 * extent
     quarter = period // 4
@@ -325,6 +325,10 @@
                 rows[d] += [total[:, :LANES], total[:, LANES:]]
         return [jnp.concatenate(rows[d], axis=0) for d in range(2)]
 
+    def fence():
+        pl.semaphore_signal(fence_sem, 1)
+        pl.semaphore_wait(fence_sem, 1)
+
     def send_kicks(section, b, parts):
         own = jnp.concatenate(parts, axis=0).astype(bf16)
         kick_src[section, b] = own
@@ -435,6 +439,8 @@
             else:
                 share = 1.0 / GROUP
                 send_last_kicks(target, [parts[d] + share * momentum[target][d] for d in range(2)])
+            if source == first:
+                fence()
         first = second
 
     for b in (1, 0):
@@ -495,6 +501,7 @@
             pltpu.VMEM((2, tiles, 8, LANES), f32),
             pltpu.VMEM((2, GROUP, 8, LANES), f32),
             dma((8,)),
+            pltpu.SemaphoreType.REGULAR,
             dma((2, planes)),
             dma((2, planes)),
             dma((SECTIONS - 1,)),

time: 57.3 us -> 51.5 us (0.90)
  the two profiles are of different devices: /device:TPU:16 before, /device:TPU:8 now
where the time goes in v5:
time: 51.5 us; the launch traced here: 51.3 us
  Pallas kernels  50 us (97%)
  local copies, waits for them, and re-layouts  1.26 us (2%)
    pallas_call x1, Pallas kernels, per_device(): pl.pallas_call(functools.partial(kernel, (columns, planes, extent, partic...  50 us
    unnamed x1, local copies, waits for them, and re-layouts  1.26 us

profile of v5, /device:TPU:8, one launch (start us, length us, event | category | flops | bytes accessed | tf_op | source)
XLA Modules:
  0.0 51.3 jit_solution(15469674198197553863)
XLA Ops:
  0.0 50.0 %shard_map.109 = f32[2,1,2,64]{3,2,1,0:T(2,128)} custom-call(s32[2,1,2,1024]{3,2,1,0:T(2,128)} %cells_ref.1, f32[2,1,2,1024]{3,2,1,0:T(2,128)} %offsets_ref.1, f32[2,1,1024]{2,1,0:T(1,128)} %charges_ref.1, f32[2,1,2,64]{3,2,1,0:T(2,128)} %momenta_ref.1, f32[1024,1024]{1,0:T(8,128)} %green_ref.1, f32[2,16,512]{2,1,0:T(8,128)} %constant.12.clone.column_hbm, ...), custom_call_target="tpu_custom_call" | custom-call | tf_op jit(solution)/shard_map/pallas_call | solution.py:469
  50.0 1.3 %copy.13 = f32[2,1,2,64]{3,2,1,0:T(2,128)} copy(f32[2,1,2,64]{3,2,1,0:T(2,128)} %shard_map.109) | data formatting | bytes 2048
